TPU v7x, 8 devices: a whole 2x2x1 slice. The times are simulated.
8 devices in a mesh: data: 8 (over z, y, x, core).
Axes of the slice: x: 2, y: 2, z: 1, core: 2. Of those that a mesh axis runs over, the one named last changes fastest.
Arguments:
- tokens: bfloat16 [16384, 512], P('data')
- d_logits: bfloat16 [16384, 32000], P('data')
- w_up: bfloat16 [2, 512, 1376], replicated
- w_down: bfloat16 [2, 1376, 512], replicated
- w_out: bfloat16 [512, 32000], replicated
- proj_up: bfloat16 [2, 512, 128], replicated
- proj_down: bfloat16 [2, 512, 128], replicated
- mom_up: float32 [2, 128, 1376], P(None, None, 'data')
- var_up: float32 [2, 128, 1376], P(None, None, 'data')
- mom_down: float32 [2, 1376, 128], P(None, 'data')
- var_down: float32 [2, 1376, 128], P(None, 'data')
- mom_out: float32 [512, 32000], P(None, 'data')
- var_out: float32 [512, 32000], P(None, 'data')
Outputs:
- output 1: bfloat16 [2, 512, 1376], replicated
- output 2: bfloat16 [2, 1376, 512], replicated
- output 3: bfloat16 [512, 32000], replicated
- output 4: float32 [2, 128, 1376], P(None, None, 'data')
- output 5: float32 [2, 128, 1376], P(None, None, 'data')
- output 6: float32 [2, 1376, 128], P(None, 'data')
- output 7: float32 [2, 1376, 128], P(None, 'data')
- output 8: float32 [512, 32000], P(None, 'data')
- output 9: float32 [512, 32000], P(None, 'data')
All inputs are finite; a program needn't handle non-finite values.
Results may differ from a plain program's by a relative error of at most 0.00413151.
Values are sent between devices in bfloat16 or wider.
A program may use at most 1 GiB of HBM per device.

v0:
```python
import functools

import jax
import jax.numpy as jnp
from jax import lax
from jax.experimental import pallas as pl
from jax.experimental.pallas import tpu as pltpu
from jax.sharding import PartitionSpec as P


BETA1 = 0.9
BETA2 = 0.999
EPS = 1e-8
STEP = 4
LR = 0.02
ALPHA = 0.5
LR_HEAD = 0.01
DATA_AXIS = 'data'
MESH = pl.DeviceIdType.MESH

BLK = 512
SUBS = 8
SHARD = 4000
RING = 6
EDGE = 96
DRING = 4

GROUP_DEST = (0, 1, 0, 1, 2, 0, 1, 2, 3, 0, 1, 2, 3, 2, 3, 3)
GROUP_PAIR = (0, 0, 1, 1, 0, 2, 2, 1, 0, 3, 3, 2, 1, 3, 2, 3)
GROUP_SEND = (0, 1, 2, 3, 4, 5, 6, 7, 0, 8, 9, 10, 0, 11, 0, 0)
BLOCKS = 64


def lookup(index, values):
    out = jnp.int32(values[-1])
    for position in range(len(values) - 1):
        out = jnp.where(index == position, jnp.int32(values[position]), out)
    return out


def gelu_tanh(values):
    return jax.nn.gelu(values, approximate=True)


def adam_update(gradient, moment_one, moment_two):
    moment_one = BETA1 * moment_one + (1.0 - BETA1) * gradient
    moment_two = BETA2 * moment_two + (1.0 - BETA2) * gradient * gradient
    direction = (moment_one / (1.0 - BETA1 ** STEP)) / (jnp.sqrt(moment_two / (1.0 - BETA2 ** STEP)) + EPS)
    return moment_one, moment_two, direction


def head_kernel(hidden_t, d_logits, w_out, mom, var, edge,
                w_left, w_right, mom_new, var_new, grad_hidden, recv_core, recv_first,
                dz_buf, wo_buf, acc, g_acc, add_core, add_first, recv_second, stage, moments, fin_w,
                dz_sem, wo_sem, core_sem, first_sem, second_sem, stage_sem, add_sem, load_sem, edge_sem, store_sem, fin_sem):
    me = lax.axis_index(DATA_AXIS)
    core = lax.rem(me, 2)
    pos_x = lax.rem(me // 2, 2)
    pos_y = me // 4
    partner = me + 1 - 2 * core
    near_x = me + 2 - 4 * pos_x
    near_y = me + 4 - 8 * pos_y

    barrier = pltpu.get_barrier_semaphore()
    for other in (partner, near_x, near_y):
        pl.semaphore_signal(barrier, inc=1, device_id=(other,), device_id_type=MESH)
    pl.semaphore_wait(barrier, 3)

    def decode(n):
        group = n // 4
        half = lax.rem(n, 2)
        own = lax.rem(n // 2, 2)
        rel = lookup(group, GROUP_DEST)
        far_first = 1 - rel // 2
        far_second = 1 - lax.rem(rel, 2)
        sub = 2 * lookup(group, GROUP_PAIR) + half
        delta_x = jnp.where(half == 0, far_first, far_second)
        delta_y = jnp.where(half == 0, far_second, far_first)
        dest_x = pos_x + delta_x - 2 * pos_x * delta_x
        dest_y = pos_y + delta_y - 2 * pos_y * delta_y
        dest_core = jnp.where(own == 1, core, 1 - core)
        dest = (dest_y * 2 + dest_x) * 2 + dest_core
        col = pl.multiple_of(((125 * dest) // 4 + 4 * sub) * 128, 128)
        return group, half, own, rel, sub, dest, col

    def fetch(n):
        col = decode(n)[-1]
        slot = lax.rem(n, 2)
        return (pltpu.make_async_copy(d_logits.at[:, pl.ds(col, BLK)], dz_buf.at[slot], dz_sem.at[slot]),
                pltpu.make_async_copy(w_out.at[:, pl.ds(col, BLK)], wo_buf.at[slot], wo_sem.at[slot]))

    def send(slot, target_ref, recv_sem, device):
        return pltpu.make_async_remote_copy(
            src_ref=stage.at[slot], dst_ref=target_ref, send_sem=stage_sem.at[slot], recv_sem=recv_sem,
            device_id=(device,), device_id_type=MESH)

    def to_core(slot, index):
        return send(slot, recv_core.at[index], core_sem.at[index], partner)

    def to_first(slot, index, device):
        return send(slot, recv_first.at[index], first_sem.at[index], device)

    def to_second(slot, index, device):
        return send(slot, recv_second.at[index], second_sem.at[index], device)

    def wait_slot(slot):
        to_core(slot, 0).wait_send()

    shift = 32 * lax.rem(me, 4)

    def moment_loads(sub, half):
        first_row = jnp.clip(BLK * sub - shift, 0, SHARD - BLK)
        place = pl.multiple_of(EDGE + first_row + shift - BLK * sub, 32)
        rows = pl.ds(pl.multiple_of(first_row, 32), BLK)
        return [pltpu.make_async_copy(source.at[rows], moments.at[half, kind, pl.ds(place, BLK)], load_sem.at[half, kind])
                for kind, source in enumerate((mom, var))]

    def edge_loads(half):
        place = pl.ds(pl.multiple_of(BLK + shift, 32), EDGE)
        return [pltpu.make_async_copy(edge.at[kind], moments.at[half, kind, place], edge_sem.at[half, kind])
                for kind in range(2)]

    def moment_stores(sub, half):
        pieces = [(None, EDGE, BLK - 2 * EDGE)]
        for step in range(3):
            pieces.append((jnp.logical_or(sub > 0, 32 * step >= shift), 32 * step, 32))
            pieces.append((jnp.logical_or(sub < SUBS - 1, 32 * step < shift), BLK - EDGE + 32 * step, 32))
        out = []
        for position, (needed, row, size) in enumerate(pieces):
            target = jnp.maximum(BLK * sub - shift + row, 0)
            rows = pl.ds(pl.multiple_of(target, 32), size)
            for kind, result in enumerate((mom_new, var_new)):
                out.append((needed, pltpu.make_async_copy(
                    moments.at[half, kind, pl.ds(EDGE + row, size)], result.at[rows], store_sem.at[half, kind, position])))
        return out

    def weight_stores(sub, half):
        cols = pl.ds(pl.multiple_of(lax.rem(sub, SUBS // 2) * BLK, BLK), BLK)
        return [(sub < SUBS // 2, pltpu.make_async_copy(fin_w.at[half], w_left.at[:, cols], fin_sem.at[half])),
                (sub >= SUBS // 2, pltpu.make_async_copy(fin_w.at[half], w_right.at[:, cols], fin_sem.at[half]))]

    def for_stores(sub, half, action):
        for needed, copy in moment_stores(sub, half) + weight_stores(sub, half):
            if needed is None:
                action(copy)
            else:
                pl.when(needed)(functools.partial(action, copy))

    for copy in fetch(jnp.int32(0)):
        copy.start()
    g_acc[...] = jnp.zeros_like(g_acc)

    def body(n, carry):
        group, half, own, rel, sub, dest, col = decode(n)
        slot = lax.rem(n, 2)

        @pl.when(n + 1 < BLOCKS)
        def _():
            for copy in fetch(n + 1):
                copy.start()

        core_index = sub * 4 + rel
        first_index = sub * 2 + 1 - lax.rem(rel, 2)
        needs_first = jnp.logical_and(own == 1, rel >= 2)
        is_final = jnp.logical_and(own == 1, rel == 3)
        load_core = pltpu.make_async_copy(recv_core.at[core_index], add_core.at[half], add_sem.at[half, 0])
        load_first = pltpu.make_async_copy(recv_first.at[first_index], add_first.at[half], add_sem.at[half, 1])

        for copy in fetch(n):
            copy.wait()

        @pl.loop(0, BLK // 256)
        def _(tile):
            cols = pl.ds(pl.multiple_of(tile * 256, 256), 256)
            acc[half, :, cols] = jnp.dot(hidden_t[...], dz_buf[slot, :, cols], preferred_element_type=jnp.float32)

        @pl.when(own == 1)
        def _():
            to_core(0, core_index).wait_recv()
            load_core.start()

        @pl.when(needs_first)
        def _():
            to_first(0, first_index, near_x).wait_recv()
            load_first.start()

        @pl.when(is_final)
        def _():
            @pl.when(sub >= 2)
            def _():
                for_stores(sub - 2, half, lambda copy: copy.wait())

            for copy in moment_loads(sub, half):
                copy.start()

            @pl.when(sub == SUBS - 1)
            def _():
                for copy in edge_loads(half):
                    copy.start()

            fin_w[half] = wo_buf[slot]

        @pl.when(own == 0)
        def _():
            place = 2 * RING + lax.rem(group, 2) * 2 + half

            @pl.when(group >= 2)
            def _():
                wait_slot(place)

            stage[place] = acc[half]
            to_core(place, core_index).start()

        turn = lookup(group, GROUP_SEND)
        along_y = jnp.where(rel < 2, half, 1 - half)
        place = along_y * RING + lax.rem(turn, RING)
        device = jnp.where(along_y == 1, near_y, near_x)

        @pl.when(jnp.logical_and(own == 1, rel < 2))
        def _():
            load_core.wait()

            @pl.when(turn >= RING)
            def _():
                wait_slot(place)

            stage[place] = acc[half] + add_core[half]
            to_first(place, first_index, device).start()

        @pl.when(jnp.logical_and(own == 1, rel == 2))
        def _():
            load_core.wait()
            load_first.wait()

            @pl.when(turn >= RING)
            def _():
                wait_slot(place)

            stage[place] = acc[half] + add_core[half] + add_first[half]
            to_second(place, sub, device).start()

        lane = lax.broadcasted_iota(jnp.int32, (1, BLK), 1) + (col - SHARD * dest)
        keep = jnp.where(jnp.logical_and(lane >= 0, lane < SHARD), 1.0, 0.0).astype(jnp.bfloat16)
        weights = wo_buf[slot] * keep

        @pl.loop(0, 4)
        def _(tile):
            rows = pl.ds(pl.multiple_of(tile * 512, 512), 512)
            g_acc[rows, :] += lax.dot_general(dz_buf[slot, rows, :], weights, (((1,), (1,)), ((), ())),
                                              preferred_element_type=jnp.float32)

        @pl.when(jnp.logical_and(is_final, half == 1))
        def _():
            for part in range(2):
                this = sub - 1 + part
                to_second(0, this, near_x).wait_recv()
                pltpu.make_async_copy(recv_core.at[this * 4 + 3], add_core.at[part], add_sem.at[part, 0]).wait()
                pltpu.make_async_copy(recv_first.at[this * 2], add_first.at[part], add_sem.at[part, 1]).wait()
                for copy in moment_loads(this, part):
                    copy.wait()

                @pl.when(this == SUBS - 1)
                def _():
                    for copy in edge_loads(part):
                        copy.wait()

            @pl.loop(0, 2 * (BLK // 128))
            def _(tile):
                part = tile // (BLK // 128)
                tile = lax.rem(tile, BLK // 128)
                cols = pl.ds(pl.multiple_of(tile * 128, 128), 128)
                rows = pl.ds(pl.multiple_of(EDGE + tile * 128, 32), 128)
                total = acc[part, :, cols] + add_core[part, :, cols] + add_first[part, :, cols] + recv_second[sub - 1 + part, :, cols]
                first, second, direction = adam_update(total.T, moments[part, 0, rows, :], moments[part, 1, rows, :])
                moments[part, 0, rows, :] = first
                moments[part, 1, rows, :] = second
                fin_w[part, :, cols] = (fin_w[part, :, cols].astype(jnp.float32) - LR_HEAD * direction.T).astype(jnp.bfloat16)

            for part in range(2):
                for_stores(sub - 1 + part, part, lambda copy: copy.start())

        return carry

    lax.fori_loop(0, BLOCKS, body, 0)

    @pl.loop(0, 4)
    def _(tile):
        rows = pl.ds(pl.multiple_of(tile * 512, 512), 512)
        grad_hidden[rows, :] = g_acc[rows, :].astype(jnp.bfloat16)

    for half in range(2):
        for_stores(SUBS - 2 + half, half, lambda copy: copy.wait())
    for place in range(2 * RING + DRING):
        wait_slot(place)


def head_update(hidden, d_logits, w_out, mom_t, var_t, edge):
    tokens, dim = hidden.shape
    f32 = jnp.float32
    bf16 = jnp.bfloat16
    any_spec = pl.BlockSpec(memory_space=pl.ANY)
    vmem = pl.BlockSpec(memory_space=pltpu.VMEM)
    outs = pl.pallas_call(
        head_kernel,
        out_shape=(
            jax.ShapeDtypeStruct((dim, SUBS * BLK // 2), bf16),
            jax.ShapeDtypeStruct((dim, SUBS * BLK // 2), bf16),
            jax.ShapeDtypeStruct(mom_t.shape, f32),
            jax.ShapeDtypeStruct(var_t.shape, f32),
            pltpu.VMEM((tokens, dim), bf16),
            jax.ShapeDtypeStruct((4 * SUBS, dim, BLK), f32),
            jax.ShapeDtypeStruct((2 * SUBS, dim, BLK), f32),
        ),
        in_specs=[vmem] + [any_spec] * 5,
        out_specs=(any_spec, any_spec, any_spec, any_spec, vmem, any_spec, any_spec),
        scratch_shapes=[
            pltpu.VMEM((2, tokens, BLK), bf16),
            pltpu.VMEM((2, dim, BLK), bf16),
            pltpu.VMEM((2, dim, BLK), f32),
            pltpu.VMEM((tokens, dim), f32),
            pltpu.VMEM((2, dim, BLK), f32),
            pltpu.VMEM((2, dim, BLK), f32),
            pltpu.VMEM((SUBS, dim, BLK), f32),
            pltpu.VMEM((2 * RING + DRING, dim, BLK), f32),
            pltpu.VMEM((2, 2, BLK + 2 * EDGE, dim), f32),
            pltpu.VMEM((2, dim, BLK), bf16),
            pltpu.SemaphoreType.DMA((2,)),
            pltpu.SemaphoreType.DMA((2,)),
            pltpu.SemaphoreType.DMA((4 * SUBS,)),
            pltpu.SemaphoreType.DMA((2 * SUBS,)),
            pltpu.SemaphoreType.DMA((SUBS,)),
            pltpu.SemaphoreType.DMA((2 * RING + DRING,)),
            pltpu.SemaphoreType.DMA((2, 2)),
            pltpu.SemaphoreType.DMA((2, 2)),
            pltpu.SemaphoreType.DMA((2, 2)),
            pltpu.SemaphoreType.DMA((2, 2, 7)),
            pltpu.SemaphoreType.DMA((2,)),
        ],
        compiler_params=pltpu.CompilerParams(collective_id=0, has_side_effects=True, vmem_limit_bytes=56 * 1024 * 1024),
        cost_estimate=pl.CostEstimate(flops=280_000_000_000, bytes_accessed=300_000_000, transcendentals=0),
        name='head_update',
    )(hidden.T, d_logits, w_out, mom_t, var_t, edge)
    return outs[:5]


def flip(me, far):
    for bit, weight in zip(far, (2, 4, 1)):
        if bit:
            me = me + weight - 2 * weight * lax.rem(me // weight, 2)
    return me


def permute(value, far):
    mask = 2 * far[0] + 4 * far[1] + far[2]
    return lax.ppermute(value, DATA_AXIS, [(dev, dev ^ mask) for dev in range(8)])


def place_kernel(origins, num_copies, has_base, *refs):
    count = len(origins)
    pieces = refs[:count]
    sources = refs[count:count + num_copies]
    refs = refs[count + num_copies + has_base:]
    out, targets = refs[0], refs[1:1 + num_copies]
    buf, in_sem, out_sem, edge_sem = refs[1 + num_copies:5 + num_copies]
    me = lax.axis_index(DATA_AXIS)
    width = pieces[0].shape[-1]
    loads = [pltpu.make_async_copy(piece, buf.at[position], in_sem.at[position]) for position, piece in enumerate(pieces)]
    for load in loads:
        load.start()
    if num_copies:
        wide, wide_in, wide_out = refs[5 + num_copies:]
        rows = wide.shape[1]
        steps = sources[0].shape[0] // rows
        work = [(kind, step) for step in range(steps) for kind in range(num_copies)]

        def wide_load(index):
            kind, step = work[index]
            return pltpu.make_async_copy(sources[kind].at[pl.ds(step * rows, rows)], wide.at[index % 4], wide_in.at[index % 4])

        def wide_store(index):
            kind, step = work[index]
            return pltpu.make_async_copy(wide.at[index % 4], targets[kind].at[pl.ds(step * rows, rows)], wide_out.at[index % 4])

        for index in range(2):
            wide_load(index).start()
        for index in range(len(work)):
            wide_load(index).wait()
            wide_store(index).start()
            if index + 2 < len(work):
                if index >= 2:
                    wide_store(index - 2).wait()
                wide_load(index + 2).start()
        for index in range(len(work) - 4, len(work)):
            wide_store(index).wait()
    stores = []
    for position, (far, part) in enumerate(origins):
        loads[position].wait()
        dest = flip(me, far)
        col = pl.multiple_of(((125 * dest) // 4) * 128 + part * width, 128)
        skip = 0 if part else 128
        store = pltpu.make_async_copy(buf.at[position, :, pl.ds(skip, width - skip)],
                                      out.at[:, pl.ds(pl.multiple_of(col + skip, 128), width - skip)], out_sem.at[position])
        store.start()
        stores.append(store)
        if not part:
            edge = pltpu.make_async_copy(buf.at[position, :, pl.ds(0, 128)], out.at[:, pl.ds(col, 128)], edge_sem.at[position])

            @pl.when(lax.rem(dest, 4) == 0)
            def _():
                edge.start()
                edge.wait()
    for store in stores:
        store.wait()


def place(base, placed, vocab, copies=()):
    pieces = [piece for piece, _, _ in placed]
    origins = tuple((far, part) for _, far, part in placed)
    dim, width = pieces[0].shape
    count = len(pieces)
    has_base = base is not None
    args = pieces + list(copies) + ([base] if has_base else [])
    scratch = [pltpu.VMEM((count, dim, width), jnp.bfloat16)] + [pltpu.SemaphoreType.DMA((count,))] * 3
    if copies:
        scratch += [pltpu.VMEM((4, 400, dim), jnp.float32), pltpu.SemaphoreType.DMA((4,)), pltpu.SemaphoreType.DMA((4,))]
    any_spec = pl.BlockSpec(memory_space=pl.ANY)
    outs = pl.pallas_call(
        functools.partial(place_kernel, origins, len(copies), int(has_base)),
        out_shape=[jax.ShapeDtypeStruct((dim, vocab), jnp.bfloat16)] + [jax.ShapeDtypeStruct(c.shape, c.dtype) for c in copies],
        in_specs=[any_spec] * len(args),
        out_specs=[any_spec] * (1 + len(copies)),
        scratch_shapes=scratch,
        input_output_aliases={len(args) - 1: 0} if has_base else {},
        compiler_params=pltpu.CompilerParams(vmem_limit_bytes=40 * 1024 * 1024),
        cost_estimate=pl.CostEstimate(flops=6_000_000_000 if copies else 3_000_000_000, bytes_accessed=count * 4 * dim * width, transcendentals=0),
        name='place',
    )(*args)
    return outs


NEAR = ((1, 0), (0, 1), (1, 1))


def small_kernel(up_0, up_1, down_0, down_1, mom, var, mom_new, var_new, dir_up, dir_down,
                 parts, dirs, whole, from_core, from_chip, stage,
                 core_send, core_recv, chip_send, chip_recv, gather_send, gather_recv, back_send, back_recv):
    me = lax.axis_index(DATA_AXIS)
    partner = flip(me, (0, 0, 1))
    chips = [me] + [flip(me, far + (0,)) for far in NEAR]
    barrier = pltpu.get_barrier_semaphore()
    for other in chips[1:] + [partner]:
        pl.semaphore_signal(barrier, inc=1, device_id=(other,), device_id_type=MESH)
    pl.semaphore_wait(barrier, 4)

    shard = parts.shape[2]
    lows = (up_0, up_1, down_0, down_1)
    for dev in range(parts.shape[0]):
        for kind, low in enumerate(lows):
            parts[dev, kind] = low[dev * shard:(dev + 1) * shard, :]

    def remote(source, target, send_sem, recv_sem, device):
        return pltpu.make_async_remote_copy(src_ref=source, dst_ref=target, send_sem=send_sem, recv_sem=recv_sem,
                                            device_id=(device,), device_id_type=MESH)

    order = (1, 2, 3, 0)
    to_core = {}
    for k in order:
        to_core[k] = remote(parts.at[flip(chips[k], (0, 0, 1))], from_core.at[k], core_send.at[k], core_recv.at[k], partner)
        to_core[k].start()
    to_chip = []
    for k in (1, 2, 3):
        to_core[k].wait_recv()
        stage[k - 1] = parts[chips[k]] + from_core[k]
        copy = remote(stage.at[k - 1], from_chip.at[k - 1], chip_send.at[k - 1], chip_recv.at[k - 1], chips[k])
        copy.start()
        to_chip.append(copy)
    to_core[0].wait_recv()
    for copy in to_chip:
        copy.wait_recv()
    total = parts[me] + from_core[0] + from_chip[0] + from_chip[1] + from_chip[2]
    first, second, direction = adam_update(total, mom[...], var[...])
    mom_new[...] = first
    var_new[...] = second
    dirs[me] = direction.astype(jnp.bfloat16)
    gather = [remote(dirs.at[me], dirs.at[me], gather_send.at[k - 1], gather_recv.at[k - 1], chips[k]) for k in (1, 2, 3)]
    back = [remote(dirs.at[chips[k]], dirs.at[chips[k]], back_send.at[k], back_recv.at[k], partner) for k in range(4)]
    for copy in gather:
        copy.start()
    back[0].start()
    for k in (1, 2, 3):
        remote(dirs.at[chips[k]], dirs.at[chips[k]], gather_send.at[k - 1], gather_recv.at[k - 1], chips[k]).wait_recv()
        back[k].start()
    for k in range(4):
        remote(dirs.at[flip(chips[k], (0, 0, 1))], dirs.at[flip(chips[k], (0, 0, 1))], back_send.at[k], back_recv.at[k], partner).wait_recv()
        back[k].wait_send()
        to_core[k].wait_send()
    for copy in gather + to_chip:
        copy.wait_send()
    for kind in range(4):
        for dev in range(parts.shape[0]):
            whole[dev * shard:(dev + 1) * shard, :] = dirs[dev, kind].astype(jnp.float32)
        target = dir_up if kind < 2 else dir_down
        target[kind % 2] = whole[...].astype(jnp.bfloat16)


def small_update(lows, mom, var):
    shape = mom.shape
    rows, rank = lows[0].shape
    devices = rows // shape[1]
    f32 = jnp.float32
    vmem = pl.BlockSpec(memory_space=pltpu.VMEM)
    dma = pltpu.SemaphoreType.DMA
    return pl.pallas_call(
        small_kernel,
        out_shape=(jax.ShapeDtypeStruct(shape, f32), jax.ShapeDtypeStruct(shape, f32),
                   jax.ShapeDtypeStruct((2, rows, rank), jnp.bfloat16), jax.ShapeDtypeStruct((2, rows, rank), jnp.bfloat16)),
        in_specs=[vmem] * 6,
        out_specs=(vmem,) * 4,
        scratch_shapes=[pltpu.VMEM((devices,) + shape, f32), pltpu.VMEM((devices,) + shape, jnp.bfloat16),
                        pltpu.VMEM((rows, rank), f32), pltpu.VMEM((4,) + shape, f32), pltpu.VMEM((3,) + shape, f32), pltpu.VMEM((3,) + shape, f32),
                        dma((4,)), dma((4,)), dma((3,)), dma((3,)), dma((3,)), dma((3,)), dma((4,)), dma((4,))],
        compiler_params=pltpu.CompilerParams(collective_id=1, has_side_effects=True, vmem_limit_bytes=32 * 1024 * 1024),
        cost_estimate=pl.CostEstimate(flops=30_000_000_000, bytes_accessed=10_000_000, transcendentals=0),
        name='small_update',
    )(*lows, mom, var)


def local_step(tokens, d_logits, w_up, w_down, w_out, proj_up, proj_down, mom_up, var_up, mom_down, var_down, mom_out, var_out):
    num_layers = w_up.shape[0]
    hidden = tokens
    saved_acts = []
    for layer_idx in range(num_layers):
        pre_act = jnp.dot(hidden, w_up[layer_idx], preferred_element_type=jnp.float32).astype(jnp.bfloat16)
        post_act = gelu_tanh(pre_act.astype(jnp.float32)).astype(jnp.bfloat16)
        saved_acts.append((hidden, pre_act, post_act))
        hidden = (hidden.astype(jnp.float32) + jnp.dot(post_act, w_down[layer_idx], preferred_element_type=jnp.float32)).astype(jnp.bfloat16)

    devices = lax.axis_size(DATA_AXIS)
    mom_t, var_t = mom_out.T, var_out.T
    edge = lax.ppermute(jnp.stack([mom_t[:EDGE], var_t[:EDGE]]), DATA_AXIS, [(dev, dev - 1) for dev in range(1, devices)])
    left, right, m_raw, v_raw, grad_hidden = head_update(hidden, d_logits, w_out, mom_t, var_t, edge)
    far_x, far_y, far_xy, near = (1, 0, 0), (0, 1, 0), (1, 1, 0), (0, 0, 0)
    left_x = permute(left, far_x)
    right_y = permute(right, far_y)

    def with_core(pieces):
        return pieces + [(permute(piece, (0, 0, 1)), (far[0], far[1], 1), part) for piece, far, part in pieces]

    ups = []
    downs = []
    for layer_idx in reversed(range(num_layers)):
        hidden_in, pre_act, post_act = saved_acts[layer_idx]
        grad_down = jnp.einsum('tf,td->fd', post_act, grad_hidden, preferred_element_type=jnp.float32)
        d_post = jnp.einsum('td,fd->tf', grad_hidden, w_down[layer_idx], preferred_element_type=jnp.float32)
        gelu_pull = jax.vjp(gelu_tanh, pre_act.astype(jnp.float32))[1]
        d_pre = gelu_pull(d_post)[0].astype(jnp.bfloat16)
        if layer_idx == num_layers - 1:
            d_pre, left, right = lax.optimization_barrier((d_pre, left, right))
            left_y = permute(left, far_y)
            right_x = permute(right, far_x)
        else:
            d_pre = lax.optimization_barrier(d_pre)
        grad_up = jnp.einsum('tf,td->fd', d_pre, hidden_in, preferred_element_type=jnp.float32)
        if layer_idx > 0:
            grad_hidden = (grad_hidden.astype(jnp.float32) + jnp.einsum('tf,df->td', d_pre, w_up[layer_idx], preferred_element_type=jnp.float32)).astype(jnp.bfloat16)
        low_up = jnp.dot(grad_up, proj_up[layer_idx].astype(jnp.float32), preferred_element_type=jnp.float32)
        low_down = jnp.dot(grad_down, proj_down[layer_idx].astype(jnp.float32), preferred_element_type=jnp.float32)
        ups.append(low_up)
        downs.append(low_down)
    ups = ups[::-1]
    downs = downs[::-1]

    vocab = d_logits.shape[1]
    ups[0], downs[0], left_x, right_y = lax.optimization_barrier((ups[0], downs[0], left_x, right_y))
    left_xy = permute(left_x, far_y)
    right_xy = permute(right_y, far_x)
    own_pieces = with_core([(left, near, 0), (right, near, 1)])
    w_new, m_out, v_out = place(None, own_pieces, vocab, (m_raw, v_raw))
    w_new, = place(w_new, with_core([(left_x, far_x, 0), (right_y, far_y, 1)]), vocab)

    w_new, left_y, right_x = lax.optimization_barrier((w_new, left_y, right_x))
    w_new, = place(w_new, with_core([(left_y, far_y, 0), (right_x, far_x, 1)]), vocab)
    first = jnp.concatenate([jnp.swapaxes(mom_up, 1, 2), mom_down], axis=0)
    second = jnp.concatenate([jnp.swapaxes(var_up, 1, 2), var_down], axis=0)
    lows = ups + downs
    w_new, lows[0] = lax.optimization_barrier((w_new, lows[0]))
    m_low, v_low, dir_up, dir_down = small_update(lows, first, second)
    m_low, left_xy, right_xy = lax.optimization_barrier((m_low, left_xy, right_xy))
    step_up = jnp.einsum('ldr,lfr->ldf', proj_up, dir_up, preferred_element_type=jnp.float32)
    step_down = jnp.einsum('lfr,ldr->lfd', dir_down, proj_down, preferred_element_type=jnp.float32)
    w_up_new = (w_up.astype(jnp.float32) - LR * ALPHA * step_up).astype(jnp.bfloat16)
    w_down_new = (w_down.astype(jnp.float32) - LR * ALPHA * step_down).astype(jnp.bfloat16)

    w_out_new, = place(w_new, with_core([(left_xy, far_xy, 0), (right_xy, far_xy, 1)]), vocab)

    return (w_up_new, w_down_new, w_out_new,
            jnp.swapaxes(m_low[:num_layers], 1, 2), jnp.swapaxes(v_low[:num_layers], 1, 2),
            m_low[num_layers:], v_low[num_layers:],
            m_out.T, v_out.T)


def solution(mesh):
    row_spec = P(DATA_AXIS, None)
    whole = P()
    up_spec = P(None, None, DATA_AXIS)
    down_spec = P(None, DATA_AXIS, None)
    head_spec = P(None, DATA_AXIS)
    in_specs = (row_spec, row_spec, whole, whole, whole, whole, whole, up_spec, up_spec, down_spec, down_spec, head_spec, head_spec)
    out_specs = (whole, whole, whole, up_spec, up_spec, down_spec, down_spec, head_spec, head_spec)
    return jax.shard_map(local_step, mesh=mesh, in_specs=in_specs, out_specs=out_specs, check_vma=False)
```

profile of v0, /device:TPU:0, one launch (start us, length us, event | category | flops | bytes accessed | tf_op | source)
XLA Modules:
  0.0 543.8 jit_solution(9229305282567106442)
XLA Ops:
  0.6 0.0 copy-start.4
  0.7 1.2 slice_bitcast_fusion
  1.9 1.3 collective-permute-start
  3.2 3.9 copy.25
  7.1 5.1 convolution_convert_fusion.1
  12.2 0.0 copy-start.18
  12.3 5.3 add_convert_fusion.2
  17.6 0.0 copy-start.21
  17.6 3.3 convolution_convert_fusion
  20.9 6.3 %fusion.21.hidden_t = bf16[512,2048]{1,0:T(8,128)(2,1)} fusion(bf16[2048,512]{0,1:T(8,128)(2,1)S(1)} %add_convert_fusion.2, bf16[2,1376,512]{2,1,0:T(8,128)(2,1)S(1)} %copy-done.7, bf16[2048,1376]{0,1:T(8,128)(2,1)S(1)} %convolution_convert_fusion), kind=kOutput, calls=%fused_computation.38 | convolution fusion | flops 2917007360 | bytes 11239424 | tf_op jit(solution)/shard_map/dot_general | solution.py:536
  27.2 0.0 collective-permute-done.edge
  27.2 301.6 %head_update.1 = (bf16[512,2048]{1,0:T(8,128)(2,1)}, bf16[512,2048]{1,0:T(8,128)(2,1)}, f32[4000,512]{1,0:T(8,128)}, f32[4000,512]{1,0:T(8,128)}, bf16[2048,512]...) custom-call(bf16[512,2048]{1,0:T(8,128)(2,1)} %fusion.21.hidden_t, ...), custom_call_target="tpu_custom_call" | custom-call | flops 280000004096 | bytes 300000000 | tf_op jit(solution)/shard_map/head_update/pallas_call | solution.py:303
  328.8 0.0 copy-start.5
  328.8 12.1 %fusion.4 = bf16[2048,1376]{0,1:T(8,128)(2,1)S(1)} fusion(bf16[2048,1376]{0,1:T(8,128)(2,1)} %copy-done.19, bf16[2048,512]{1,0:T(8,128)(2,1)S(1)} %get-tuple-element.36, bf16[2,1376,512]{2,1,0:T(8,128)(2,1)S(1)} %copy-done.8), kind=kOutput, calls=%fused_computation.14 | convolution fusion | flops 2944860160 | bytes 14778368 | tf_op jit(solution)/shard_map/td,fd->tf/dot_general | solution.py:554
  340.9 0.9 collective-permute-start.1
  341.8 1.1 collective-permute-start.2
  342.9 4.0 add_convert_fusion
  346.9 0.0 copy-start.22
  346.9 0.0 copy-start.14
  347.0 10.5 %fusion.7 = bf16[2048,1376]{0,1:T(8,128)(2,1)} fusion(bf16[2048,1376]{0,1:T(8,128)(2,1)S(1)} %bitcast.80, bf16[2048,512]{1,0:T(8,128)(2,1)S(1)} %add_convert_fusion, bf16[2,1376,512]{2,1,0:T(8,128)(2,1)S(1)} %copy-done.9), kind=kOutput, calls=%fused_computation.17 | convolution fusion | flops 2944860160 | bytes 14778368 | tf_op jit(solution)/shard_map/td,fd->tf/dot_general | solution.py:554
  357.5 0.0 copy-start.12
  357.5 0.0 collective-permute-start.5
  357.5 0.5 collective-permute-start.6
  358.0 9.1 %fusion.28.down_0 = f32[1376,128]{1,0:T(8,128)} fusion(bf16[2048,512]{1,0:T(8,128)(2,1)} %copy-done.22, bf16[2,512,128]{2,1,0:T(8,128)(2,1)S(1)} %copy-done.14, bf16[2048,1376]{0,1:T(8,128)(2,1)} %copy-done.18), kind=kOutput, calls=%fused_computation.43 | convolution fusion | flops 3094216704 | bytes 8568832 | tf_op jit(solution)/shard_map/dot_general | solution.py:567
  367.1 6.9 %fusion.31.up_0 = f32[1376,128]{1,0:T(8,128)S(1)} fusion(bf16[2048,1376]{0,1:T(8,128)(2,1)} %fusion.7, bf16[2048,512]{1,0:T(8,128)(2,1)} %param.13, bf16[2,512,128]{2,1,0:T(8,128)(2,1)S(1)} %copy-done.12), kind=kOutput, calls=%fused_computation.45 | convolution fusion | flops 3066036224 | bytes 8568832 | tf_op jit(solution)/shard_map/dot_general | solution.py:566
  374.0 14.9 %collective-permute-done.1.refs_0_ = bf16[512,2048]{1,0:T(8,128)(2,1)S(1)} collective-permute-done((bf16[512,2048]{1,0:T(8,128)(2,1)}, bf16[512,2048]{1,0:T(8,128)(2,1)S(1)}, u32[]{:S(2)}, u32[]{:S(2)}) %collective-permute-start.1) | collective-permute-done | bytes 2097184 | tf_op jit(solution)/shard_map/ppermute | solution.py:355
  388.9 0.2 collective-permute-done.2.refs_1_
  389.1 0.5 collective-permute-start.4
  389.6 1.7 collective-permute-start.7
  391.3 0.0 collective-permute-done.5.refs_2_
  391.3 0.3 collective-permute-start.8
  391.7 0.9 copy.29
  392.6 0.9 copy.31
  393.5 0.1 pad_maximum_fusion.1
  393.6 0.0 collective-permute-done.6.refs_3_
  393.6 22.3 %place.4 = (bf16[512,32000]{1,0:T(8,128)(2,1)}, f32[4000,512]{1,0:T(8,128)}, f32[4000,512]{1,0:T(8,128)}) custom-call(bf16[512,2048]{1,0:T(8,128)(2,1)} %get-tuple-element.42.refs_0_, bf16[512,2048]{1,0:T(8,128)(2,1)} %get-tuple-element.43.refs_1_, bf16[512,2048]{1,0:T(8,128)(2,1)} %collective-permute-done.5.refs_2_, ...), custom_call_target="tpu_custom_call" | custom-call | flops 6000000000 | bytes 16777216 | tf_op jit(solution)/shard_map/place/pallas_call | solution.py:427
  415.9 0.0 collective-permute-done.4.refs_3_
  415.9 4.8 place.5.refs_4_
  420.7 16.8 %collective-permute-done.7.refs_0_ = bf16[512,2048]{1,0:T(8,128)(2,1)} collective-permute-done((bf16[512,2048]{1,0:T(8,128)(2,1)}, bf16[512,2048]{1,0:T(8,128)(2,1)}, u32[]{:S(2)}, u32[]{:S(2)}) %collective-permute-start.7) | collective-permute-done | bytes 2097184 | tf_op jit(solution)/shard_map/ppermute | solution.py:355
  437.4 1.4 collective-permute-done.8.refs_1_
  438.9 0.0 collective-permute-start.9
  438.9 0.5 collective-permute-start.10
  439.4 7.7 %fusion.25.up_1 = f32[1376,128]{1,0:T(8,128)} fusion(bf16[2048,1376]{0,1:T(8,128)(2,1)} %copy-done.20, bf16[2048,512]{0,1:T(8,128)(2,1)} %copy-done.21, bf16[2,512,128]{2,1,0:T(8,128)(2,1)} %param.18), kind=kOutput, calls=%fused_computation.41 | convolution fusion | flops 3066036224 | bytes 8568832 | tf_op jit(solution)/shard_map/dot_general | solution.py:566
  447.1 9.1 %fusion.22.down_1 = f32[1376,128]{1,0:T(8,128)} fusion(bf16[2048,512]{1,0:T(8,128)(2,1)} %copy-done, bf16[2,512,128]{2,1,0:T(8,128)(2,1)} %param.19, bf16[2048,1376]{0,1:T(8,128)(2,1)} %copy-done.19), kind=kOutput, calls=%fused_computation.39 | convolution fusion | flops 3094216704 | bytes 8568832 | tf_op jit(solution)/shard_map/dot_general | solution.py:567
  456.1 0.3 collective-permute-start.11
  456.5 1.7 collective-permute-start.12
  458.2 6.4 %place.6.refs_4_ = bf16[512,32000]{1,0:T(8,128)(2,1)} custom-call(bf16[512,2048]{1,0:T(8,128)(2,1)} %collective-permute-done.7.refs_0_, bf16[512,2048]{1,0:T(8,128)(2,1)} %collective-permute-done.8.refs_1_, bf16[512,2048]{1,0:T(8,128)(2,1)} %collective-permute-done.9.refs_2_, ...), custom_call_target="tpu_custom_call", output_to_operand_aliasing={{}: (4, {})} | custom-call | flops 3000000000 | bytes 16777216 | tf_op jit(solution)/shard_map/place/pallas_call | solution.py:427
  464.6 0.0 copy-start.6
  464.6 0.0 copy-start.13
  464.7 66.3 %small_update.1 = (f32[4,172,128]{2,1,0:T(8,128)S(1)}, f32[4,172,128]{2,1,0:T(8,128)S(1)}, bf16[2,1376,128]{2,1,0:T(8,128)(2,1)S(1)}, bf16[2,1376,128]{2,1,0:T(8,128)(2,1)S(1)}) custom-call(f32[1376,128]{1,0:T(8,128)S(1)} %fusion.31.up_0, f32[1376,128]{1,0:T(8,128)S(1)} %copy-done.1, f32[1376,128]{1,0:T(8,128)S(1)} %copy-done.2, f32[1376,128]{1,0:T(8,128)S(1)} %copy-done.3, ...), custom_call_target="tpu_custom_call" | custom-call | flops 30000001024 | bytes 10000000 | tf_op jit(solution)/shard_map/small_update/pallas_call | solution.py:513
  531.0 0.0 copy-start.10
  531.0 0.0 copy-start.15
  531.0 0.0 collective-permute-done.11.refs_0_
  531.0 0.4 collective-permute-start.13
  531.4 0.1 collective-permute-start.14
  531.6 0.8 copy.34
  532.3 0.8 copy.32
  533.1 0.8 copy.35
  533.9 0.8 copy.33
  534.7 2.5 fusion.20
  537.1 2.5 subtract_convert_fusion
  539.6 0.0 collective-permute-done.13.refs_2_
  539.6 0.0 collective-permute-done.14.refs_3_
  539.6 4.0 place.7
  (50 shorter events, 0.2 us)
Async XLA Ops:
  0.6 6.5 %copy-start.4 = (bf16[2,512,1376]{1,2,0:T(8,128)(2,1)S(1)}, bf16[2,512,1376]{1,2,0:T(8,128)(2,1)}, u32[]{:S(2)}) copy-start(bf16[2,512,1376]{1,2,0:T(8,128)(2,1)} %param.15) | copy-start | bytes 8454148
  1.9 25.3 %collective-permute-start = (f32[2,96,512]{2,1,0:T(8,128)S(1)}, f32[2,96,512]{2,1,0:T(8,128)}, u32[]{:S(2)}, u32[]{:S(2)}) collective-permute-start(f32[2,96,512]{2,1,0:T(8,128)S(1)} %pad_maximum_fusion), channel_id=1, source_target_pairs={{1,0},{2,1},{3,2},{4,3},{5,4},{6,5},{7,6}} | collective-permute-start | bytes 1179656 | tf_op jit(solution)/shard_map/ppermute | solution.py:540
  7.1 5.1 copy-start.7
  7.1 5.1 copy-start.11
  12.2 5.3 copy-start.18
  17.6 3.3 copy-start.21
  20.9 6.3 %copy-start.19 = (bf16[2048,1376]{0,1:T(8,128)(2,1)}, bf16[2048,1376]{0,1:T(8,128)(2,1)S(1)}, u32[]{:S(2)}) copy-start(bf16[2048,1376]{0,1:T(8,128)(2,1)S(1)} %convolution_convert_fusion) | copy-start | bytes 16908292
  27.2 301.6 %copy-start.8 = (bf16[2,1376,512]{2,1,0:T(8,128)(2,1)S(1)}, bf16[2,1376,512]{2,1,0:T(8,128)(2,1)}, u32[]{:S(2)}) copy-start(bf16[2,1376,512]{2,1,0:T(8,128)(2,1)} %param.16) | copy-start | bytes 8454148
  328.8 14.1 %copy-start = (bf16[2048,512]{1,0:T(8,128)(2,1)}, bf16[2048,512]{1,0:T(8,128)(2,1)S(1)}, u32[]{:S(2)}) copy-start(bf16[2048,512]{1,0:T(8,128)(2,1)S(1)} %get-tuple-element.36) | copy-start | bytes 6291460
  328.8 14.1 %copy-start.5 = (bf16[2,512,1376]{1,2,0:T(8,128)(2,1)S(1)}, bf16[2,512,1376]{1,2,0:T(8,128)(2,1)}, u32[]{:S(2)}) copy-start(bf16[2,512,1376]{1,2,0:T(8,128)(2,1)} %param.15) | copy-start | bytes 8454148
  340.9 6.0 %copy-start.20 = (bf16[2048,1376]{0,1:T(8,128)(2,1)}, bf16[2048,1376]{0,1:T(8,128)(2,1)S(1)}, u32[]{:S(2)}) copy-start(bf16[2048,1376]{0,1:T(8,128)(2,1)S(1)} %fusion.4) | copy-start | bytes 16908292
  340.9 48.0 %collective-permute-start.1 = (bf16[512,2048]{1,0:T(8,128)(2,1)}, bf16[512,2048]{1,0:T(8,128)(2,1)S(1)}, u32[]{:S(2)}, u32[]{:S(2)}) collective-permute-start(bf16[512,2048]{1,0:T(8,128)(2,1)} %get-tuple-element.42.refs_0_), channel_id=1, source_target_pairs={{0,2},{1,3},{2,0},{3,1},{4,6},{5,7},{6,4},{7,5}} | collective-permute-start | bytes 6291464 | tf_op jit(solution)/shard_map/ppermute | solution.py:355
  341.8 5.1 slice-start
  341.8 5.1 copy-start.9
  341.8 5.1 slice-start.1
  341.8 47.3 %collective-permute-start.2 = (bf16[512,2048]{1,0:T(8,128)(2,1)}, bf16[512,2048]{1,0:T(8,128)(2,1)}, u32[]{:S(2)}, u32[]{:S(2)}) collective-permute-start(bf16[512,2048]{1,0:T(8,128)(2,1)} %get-tuple-element.43.refs_1_), channel_id=1, source_target_pairs={{0,4},{1,5},{2,6},{3,7},{4,0},{5,1},{6,2},{7,3}} | collective-permute-start | bytes 6291464 | tf_op jit(solution)/shard_map/ppermute | solution.py:355
  346.9 10.5 %copy-start.22 = (bf16[2048,512]{1,0:T(8,128)(2,1)}, bf16[2048,512]{1,0:T(8,128)(2,1)S(1)}, u32[]{:S(2)}) copy-start(bf16[2048,512]{1,0:T(8,128)(2,1)S(1)} %add_convert_fusion) | copy-start | bytes 6291460
  346.9 11.1 %copy-start.14 = (bf16[2,512,128]{2,1,0:T(8,128)(2,1)S(1)}, bf16[2,512,128]{2,1,0:T(8,128)(2,1)}, u32[]{:S(2)}) copy-start(bf16[2,512,128]{2,1,0:T(8,128)(2,1)} %param.19) | copy-start | bytes 786436
  357.5 9.6 %copy-start.12 = (bf16[2,512,128]{2,1,0:T(8,128)(2,1)S(1)}, bf16[2,512,128]{2,1,0:T(8,128)(2,1)}, u32[]{:S(2)}) copy-start(bf16[2,512,128]{2,1,0:T(8,128)(2,1)} %param.18) | copy-start | bytes 786436
  357.5 33.8 %collective-permute-start.5 = (bf16[512,2048]{1,0:T(8,128)(2,1)}, bf16[512,2048]{1,0:T(8,128)(2,1)}, u32[]{:S(2)}, u32[]{:S(2)}) collective-permute-start(bf16[512,2048]{1,0:T(8,128)(2,1)} %get-tuple-element.42.refs_0_), channel_id=1, source_target_pairs={{0,1},{1,0},{2,3},{3,2},{4,5},{5,4},{6,7},{7,6}} | collective-permute-start | bytes 6291464 | tf_op jit(solution)/shard_map/ppermute | solution.py:355
  357.5 36.1 %collective-permute-start.6 = (bf16[512,2048]{1,0:T(8,128)(2,1)}, bf16[512,2048]{1,0:T(8,128)(2,1)}, u32[]{:S(2)}, u32[]{:S(2)}) collective-permute-start(bf16[512,2048]{1,0:T(8,128)(2,1)} %get-tuple-element.43.refs_1_), channel_id=1, source_target_pairs={{0,1},{1,0},{2,3},{3,2},{4,5},{5,4},{6,7},{7,6}} | collective-permute-start | bytes 6291464 | tf_op jit(solution)/shard_map/ppermute | solution.py:355
  367.1 24.5 %copy-start.16 = (f32[2,128,172]{1,0,2:T(2,128)S(1)}, f32[2,128,172]{1,0,2:T(2,128)}, u32[]{:S(2)}) copy-start(f32[2,128,172]{1,0,2:T(2,128)} %param.20) | copy-start | bytes 528388
  367.1 24.5 %copy-start.17 = (f32[2,128,172]{1,0,2:T(2,128)S(1)}, f32[2,128,172]{1,0,2:T(2,128)}, u32[]{:S(2)}) copy-start(f32[2,128,172]{1,0,2:T(2,128)} %param.21) | copy-start | bytes 528388
  389.1 26.8 %collective-permute-start.3 = (bf16[512,2048]{1,0:T(8,128)(2,1)S(1)}, bf16[512,2048]{1,0:T(8,128)(2,1)S(1)}, u32[]{:S(2)}, u32[]{:S(2)}) collective-permute-start(bf16[512,2048]{1,0:T(8,128)(2,1)S(1)} %collective-permute-done.1.refs_0_), channel_id=1, source_target_pairs={{0,1},{1,0},{2,3},{3,2},{4,5},{5,4},{6,7},{7,6}} | collective-permute-start | bytes 6291464 | tf_op jit(solution)/shard_map/ppermute | solution.py:355
  389.1 26.8 %collective-permute-start.4 = (bf16[512,2048]{1,0:T(8,128)(2,1)}, bf16[512,2048]{1,0:T(8,128)(2,1)S(1)}, u32[]{:S(2)}, u32[]{:S(2)}) collective-permute-start(bf16[512,2048]{1,0:T(8,128)(2,1)} %collective-permute-done.2.refs_1_), channel_id=1, source_target_pairs={{0,1},{1,0},{2,3},{3,2},{4,5},{5,4},{6,7},{7,6}} | collective-permute-start | bytes 6291464 | tf_op jit(solution)/shard_map/ppermute | solution.py:355
  389.6 47.9 %collective-permute-start.7 = (bf16[512,2048]{1,0:T(8,128)(2,1)}, bf16[512,2048]{1,0:T(8,128)(2,1)}, u32[]{:S(2)}, u32[]{:S(2)}) collective-permute-start(bf16[512,2048]{1,0:T(8,128)(2,1)} %get-tuple-element.42.refs_0_), channel_id=1, source_target_pairs={{0,4},{1,5},{2,6},{3,7},{4,0},{5,1},{6,2},{7,3}} | collective-permute-start | bytes 6291464 | tf_op jit(solution)/shard_map/ppermute | solution.py:355
  391.3 47.6 %collective-permute-start.8 = (bf16[512,2048]{1,0:T(8,128)(2,1)}, bf16[512,2048]{1,0:T(8,128)(2,1)}, u32[]{:S(2)}, u32[]{:S(2)}) collective-permute-start(bf16[512,2048]{1,0:T(8,128)(2,1)} %get-tuple-element.43.refs_1_), channel_id=1, source_target_pairs={{0,2},{1,3},{2,0},{3,1},{4,6},{5,7},{6,4},{7,5}} | collective-permute-start | bytes 6291464 | tf_op jit(solution)/shard_map/ppermute | solution.py:355
  438.9 19.3 %collective-permute-start.9 = (bf16[512,2048]{1,0:T(8,128)(2,1)}, bf16[512,2048]{1,0:T(8,128)(2,1)}, u32[]{:S(2)}, u32[]{:S(2)}) collective-permute-start(bf16[512,2048]{1,0:T(8,128)(2,1)} %collective-permute-done.7.refs_0_), channel_id=1, source_target_pairs={{0,1},{1,0},{2,3},{3,2},{4,5},{5,4},{6,7},{7,6}} | collective-permute-start | bytes 6291464 | tf_op jit(solution)/shard_map/ppermute | solution.py:355
  438.9 19.3 %collective-permute-start.10 = (bf16[512,2048]{1,0:T(8,128)(2,1)}, bf16[512,2048]{1,0:T(8,128)(2,1)}, u32[]{:S(2)}, u32[]{:S(2)}) collective-permute-start(bf16[512,2048]{1,0:T(8,128)(2,1)} %collective-permute-done.8.refs_1_), channel_id=1, source_target_pairs={{0,1},{1,0},{2,3},{3,2},{4,5},{5,4},{6,7},{7,6}} | collective-permute-start | bytes 6291464 | tf_op jit(solution)/shard_map/ppermute | solution.py:355
  456.1 8.5 %copy-start.1 = (f32[1376,128]{1,0:T(8,128)S(1)}, f32[1376,128]{1,0:T(8,128)}, u32[]{:S(2)}) copy-start(f32[1376,128]{1,0:T(8,128)} %fusion.25.up_1) | copy-start | bytes 2113540
  456.1 8.5 %copy-start.2 = (f32[1376,128]{1,0:T(8,128)S(1)}, f32[1376,128]{1,0:T(8,128)}, u32[]{:S(2)}) copy-start(f32[1376,128]{1,0:T(8,128)} %fusion.28.down_0) | copy-start | bytes 2113540
  456.1 8.5 %copy-start.3 = (f32[1376,128]{1,0:T(8,128)S(1)}, f32[1376,128]{1,0:T(8,128)}, u32[]{:S(2)}) copy-start(f32[1376,128]{1,0:T(8,128)} %fusion.22.down_1) | copy-start | bytes 2113540
  456.1 74.9 %collective-permute-start.11 = (bf16[512,2048]{1,0:T(8,128)(2,1)S(1)}, bf16[512,2048]{1,0:T(8,128)(2,1)S(1)}, u32[]{:S(2)}, u32[]{:S(2)}) collective-permute-start(bf16[512,2048]{1,0:T(8,128)(2,1)S(1)} %collective-permute-done.1.refs_0_), channel_id=1, source_target_pairs={{0,4},{1,5},{2,6},{3,7},{4,0},{5,1},{6,2},{7,3}} | collective-permute-start | bytes 6291464 | tf_op jit(solution)/shard_map/ppermute | solution.py:355
  456.5 74.5 %collective-permute-start.12 = (bf16[512,2048]{1,0:T(8,128)(2,1)}, bf16[512,2048]{1,0:T(8,128)(2,1)S(1)}, u32[]{:S(2)}, u32[]{:S(2)}) collective-permute-start(bf16[512,2048]{1,0:T(8,128)(2,1)} %collective-permute-done.2.refs_1_), channel_id=1, source_target_pairs={{0,2},{1,3},{2,0},{3,1},{4,6},{5,7},{6,4},{7,5}} | collective-permute-start | bytes 6291464 | tf_op jit(solution)/shard_map/ppermute | solution.py:355
  464.6 70.0 %copy-start.6 = (bf16[2,512,1376]{1,2,0:T(8,128)(2,1)S(1)}, bf16[2,512,1376]{1,2,0:T(8,128)(2,1)}, u32[]{:S(2)}) copy-start(bf16[2,512,1376]{1,2,0:T(8,128)(2,1)} %param.15) | copy-start | bytes 8454148
  464.6 70.0 %copy-start.13 = (bf16[2,512,128]{2,1,0:T(8,128)(2,1)S(1)}, bf16[2,512,128]{2,1,0:T(8,128)(2,1)}, u32[]{:S(2)}) copy-start(bf16[2,512,128]{2,1,0:T(8,128)(2,1)} %param.18) | copy-start | bytes 786436
  531.0 6.1 %copy-start.10 = (bf16[2,1376,512]{2,1,0:T(8,128)(2,1)S(1)}, bf16[2,1376,512]{2,1,0:T(8,128)(2,1)}, u32[]{:S(2)}) copy-start(bf16[2,1376,512]{2,1,0:T(8,128)(2,1)} %param.16) | copy-start | bytes 8454148
  531.0 6.1 %copy-start.15 = (bf16[2,512,128]{2,1,0:T(8,128)(2,1)S(1)}, bf16[2,512,128]{2,1,0:T(8,128)(2,1)}, u32[]{:S(2)}) copy-start(bf16[2,512,128]{2,1,0:T(8,128)(2,1)} %param.19) | copy-start | bytes 786436
  531.0 8.6 %collective-permute-start.13 = (bf16[512,2048]{1,0:T(8,128)(2,1)S(1)}, bf16[512,2048]{1,0:T(8,128)(2,1)S(1)}, u32[]{:S(2)}, u32[]{:S(2)}) collective-permute-start(bf16[512,2048]{1,0:T(8,128)(2,1)S(1)} %collective-permute-done.11.refs_0_), channel_id=1, source_target_pairs={{0,1},{1,0},{2,3},{3,2},{4,5},{5,4},{6,7},{7,6}} | collective-permute-start | bytes 6291464 | tf_op jit(solution)/shard_map/ppermute | solution.py:355
  531.4 8.2 %collective-permute-start.14 = (bf16[512,2048]{1,0:T(8,128)(2,1)S(1)}, bf16[512,2048]{1,0:T(8,128)(2,1)S(1)}, u32[]{:S(2)}, u32[]{:S(2)}) collective-permute-start(bf16[512,2048]{1,0:T(8,128)(2,1)S(1)} %collective-permute-done.12.refs_1_), channel_id=1, source_target_pairs={{0,1},{1,0},{2,3},{3,2},{4,5},{5,4},{6,7},{7,6}} | collective-permute-start | bytes 6291464 | tf_op jit(solution)/shard_map/ppermute | solution.py:355
where the time goes:
time: 553 us; the launch traced here: 544 us
  Pallas kernels  405 us (73%)
  matrix products  84.1 us (15%)
  waiting for transfers between devices  33.3 us (6%)
  local copies, waits for them, and re-layouts  10.2 us (2%)
  starting transfers between devices  9.41 us (2%)
    pallas_call x1, Pallas kernels, head_update(): pl.pallas_call(head_kernel, out_shape=(jax.ShapeDtypeStruct((dim, SUBS *...  302 us
    pallas_call x1, Pallas kernels, small_update(): pl.pallas_call(small_kernel, out_shape=(jax.ShapeDtypeStruct(shape, f32),...  66.3 us
    pallas_call x4, Pallas kernels, place(): pl.pallas_call(functools.partial(place_kernel, origins, len(copies), int(...  37.4 us
    ppermute x14, waiting for transfers between devices, permute(): lax.ppermute(value, DATA_AXIS, [(dev, dev ^ mask) for dev in range(8)])  33.3 us
    dot_general x2, matrix products, local_step(): jnp.einsum('td,fd->tf', grad_hidden, w_down[layer_idx], preferred_element...  22.5 us
    dot_general x2, matrix products, local_step(): jnp.dot(grad_down, proj_down[layer_idx].astype(jnp.float32), preferred_el...  18.2 us
    dot_general x2, matrix products, local_step(): jnp.dot(grad_up, proj_up[layer_idx].astype(jnp.float32), preferred_elemen...  14.6 us
    dot_general x2, matrix products, local_step(): jnp.dot(post_act, w_down[layer_idx], preferred_element_type=jnp.float32)  11.6 us
  transfers between devices with their start and end apart: 15, of which 4 were waited for; matrix products, arithmetic and copies ran while one was open for 15% of the time, Pallas kernels for 18%

commit v1 on v0

--- a/solution.py
+++ b/solution.py
@@ -49,9 +49,9 @@
     return moment_one, moment_two, direction
 
 
-def head_kernel(hidden_t, d_logits, w_out, mom, var, edge,
+def head_kernel(hidden, d_logits, w_out, mom, var, edge,
                 w_left, w_right, mom_new, var_new, grad_hidden, recv_core, recv_first,
-                dz_buf, wo_buf, acc, g_acc, add_core, add_first, recv_second, stage, moments, fin_w,
+                hidden_t, dz_buf, wo_buf, acc, g_acc, add_core, add_first, recv_second, stage, moments, fin_w,
                 dz_sem, wo_sem, core_sem, first_sem, second_sem, stage_sem, add_sem, load_sem, edge_sem, store_sem, fin_sem):
     me = lax.axis_index(DATA_AXIS)
     core = lax.rem(me, 2)
@@ -60,11 +60,6 @@
     partner = me + 1 - 2 * core
     near_x = me + 2 - 4 * pos_x
     near_y = me + 4 - 8 * pos_y
-
-    barrier = pltpu.get_barrier_semaphore()
-    for other in (partner, near_x, near_y):
-        pl.semaphore_signal(barrier, inc=1, device_id=(other,), device_id_type=MESH)
-    pl.semaphore_wait(barrier, 3)
 
     def decode(n):
         group = n // 4
@@ -148,7 +143,18 @@
 
     for copy in fetch(jnp.int32(0)):
         copy.start()
+    barrier = pltpu.get_barrier_semaphore()
+    for other in (partner, near_x, near_y):
+        pl.semaphore_signal(barrier, inc=1, device_id=(other,), device_id_type=MESH)
+
+    @pl.loop(0, hidden.shape[0] // 512)
+    def _(tile):
+        rows = pl.ds(pl.multiple_of(tile * 512, 512), 512)
+        hidden_t[:, rows] = hidden[rows, :].T
+
     g_acc[...] = jnp.zeros_like(g_acc)
+    pl.semaphore_wait(barrier, 3)
+
 
     def body(n, carry):
         group, half, own, rel, sub, dest, col = decode(n)
@@ -166,6 +172,16 @@
         load_core = pltpu.make_async_copy(recv_core.at[core_index], add_core.at[half], add_sem.at[half, 0])
         load_first = pltpu.make_async_copy(recv_first.at[first_index], add_first.at[half], add_sem.at[half, 1])
 
+        @pl.when(own == 1)
+        def _():
+            to_core(0, core_index).wait_recv()
+            load_core.start()
+
+        @pl.when(needs_first)
+        def _():
+            to_first(0, first_index, near_x).wait_recv()
+            load_first.start()
+
         for copy in fetch(n):
             copy.wait()
 
@@ -173,16 +189,6 @@
         def _(tile):
             cols = pl.ds(pl.multiple_of(tile * 256, 256), 256)
             acc[half, :, cols] = jnp.dot(hidden_t[...], dz_buf[slot, :, cols], preferred_element_type=jnp.float32)
-
-        @pl.when(own == 1)
-        def _():
-            to_core(0, core_index).wait_recv()
-            load_core.start()
-
-        @pl.when(needs_first)
-        def _():
-            to_first(0, first_index, near_x).wait_recv()
-            load_first.start()
 
         @pl.when(is_final)
         def _():
@@ -314,6 +320,7 @@
         in_specs=[vmem] + [any_spec] * 5,
         out_specs=(any_spec, any_spec, any_spec, any_spec, vmem, any_spec, any_spec),
         scratch_shapes=[
+            pltpu.VMEM((dim, tokens), bf16),
             pltpu.VMEM((2, tokens, BLK), bf16),
             pltpu.VMEM((2, dim, BLK), bf16),
             pltpu.VMEM((2, dim, BLK), f32),
@@ -339,7 +346,7 @@
         compiler_params=pltpu.CompilerParams(collective_id=0, has_side_effects=True, vmem_limit_bytes=56 * 1024 * 1024),
         cost_estimate=pl.CostEstimate(flops=280_000_000_000, bytes_accessed=300_000_000, transcendentals=0),
         name='head_update',
-    )(hidden.T, d_logits, w_out, mom_t, var_t, edge)
+    )(hidden, d_logits, w_out, mom_t, var_t, edge)
     return outs[:5]
 
 

time: 553 us -> 544 us (0.984); the launches traced: 544 us -> 541 us
  transfers between devices with their start and end apart: 15 -> 15, of which waited for: 4 -> 4; matrix products, arithmetic and copies ran while one was open for 15% -> 14% of each run, Pallas kernels for 18% -> 19%
where the time goes in v1:
time: 544 us; the launch traced here: 541 us
  Pallas kernels  403 us (74%)
  matrix products  83.9 us (15%)
  waiting for transfers between devices  34.4 us (6%)
  local copies, waits for them, and re-layouts  9.39 us (2%)
  starting transfers between devices  8.55 us (2%)
    pallas_call x1, Pallas kernels, head_update(): pl.pallas_call(head_kernel, out_shape=(jax.ShapeDtypeStruct((dim, SUBS *...  299 us
    pallas_call x1, Pallas kernels, small_update(): pl.pallas_call(small_kernel, out_shape=(jax.ShapeDtypeStruct(shape, f32),...  66.8 us
    pallas_call x4, Pallas kernels, place(): pl.pallas_call(functools.partial(place_kernel, origins, len(copies), int(...  37.4 us
    ppermute x14, waiting for transfers between devices, permute(): lax.ppermute(value, DATA_AXIS, [(dev, dev ^ mask) for dev in range(8)])  34.4 us
    dot_general x2, matrix products, local_step(): jnp.einsum('td,fd->tf', grad_hidden, w_down[layer_idx], preferred_element...  21.7 us
    dot_general x2, matrix products, local_step(): jnp.dot(grad_down, proj_down[layer_idx].astype(jnp.float32), preferred_el...  18.2 us
    dot_general x2, matrix products, local_step(): jnp.dot(grad_up, proj_up[layer_idx].astype(jnp.float32), preferred_elemen...  14.5 us
    dot_general x2, matrix products, local_step(): jnp.dot(post_act, w_down[layer_idx], preferred_element_type=jnp.float32)  12 us
  transfers between devices with their start and end apart: 15, of which 4 were waited for; matrix products, arithmetic and copies ran while one was open for 14% of the time, Pallas kernels for 19%

profile of v1, /device:TPU:0, one launch (start us, length us, event | category | flops | bytes accessed | tf_op | source)
XLA Modules:
  0.0 540.9 jit_solution(8380600416995186963)
XLA Ops:
  0.6 1.1 slice_bitcast_fusion
  1.7 0.0 copy-start.7
  1.7 0.0 copy-start.17
  1.8 1.6 collective-permute-start
  3.3 5.1 convolution_convert_fusion.1
  8.4 0.0 copy-start.20
  8.4 2.5 copy-done.20
  10.9 5.8 %add_convert_fusion.2 = bf16[2048,512]{1,0:T(8,128)(2,1)S(1)} fusion(bf16[2048,512]{1,0:T(8,128)(2,1)S(1)} %copy-done.17, bf16[2,1376,512]{2,1,0:T(8,128)(2,1)S(1)} %copy-done.7, bf16[2048,1376]{0,1:T(8,128)(2,1)S(1)} %convolution_convert_fusion.1), kind=kOutput, calls=%fused_computation.37 | convolution fusion | flops 2917007360 | bytes 11239424 | tf_op jit(solution)/shard_map/dot_general | solution.py:543
  16.7 0.0 copy-start.22
  16.7 3.3 convolution_convert_fusion
  20.1 6.3 %add_convert_fusion.1.hidden = bf16[2048,512]{1,0:T(8,128)(2,1)} fusion(bf16[2048,512]{1,0:T(8,128)(2,1)S(1)} %add_convert_fusion.2, bf16[2,1376,512]{2,1,0:T(8,128)(2,1)S(1)} %copy-done.7, bf16[2048,1376]{0,1:T(8,128)(2,1)S(1)} %convolution_convert_fusion), kind=kOutput, calls=%fused_computation.36 | convolution fusion | flops 2917007360 | bytes 11239424 | tf_op jit(solution)/shard_map/dot_general | solution.py:543
  26.4 0.0 collective-permute-done.edge
  26.4 0.7 copy-done.18
  27.1 298.9 %head_update.1 = (bf16[512,2048]{1,0:T(8,128)(2,1)}, bf16[512,2048]{1,0:T(8,128)(2,1)}, f32[4000,512]{1,0:T(8,128)}, f32[4000,512]{1,0:T(8,128)}, bf16[2048,512]...) custom-call(bf16[2048,512]{1,0:T(8,128)(2,1)} %add_convert_fusion.1.hidden, ...), custom_call_target="tpu_custom_call" | custom-call | flops 280000004096 | bytes 300000000 | tf_op jit(solution)/shard_map/head_update/pallas_call | solution.py:309
  326.1 0.0 copy-start.5
  326.1 11.4 %fusion.4 = bf16[2048,1376]{0,1:T(8,128)(2,1)S(1)} fusion(bf16[2048,1376]{0,1:T(8,128)(2,1)} %copy-done.19, bf16[2048,512]{1,0:T(8,128)(2,1)S(1)} %get-tuple-element.36, bf16[2,1376,512]{2,1,0:T(8,128)(2,1)S(1)} %copy-done.8), kind=kOutput, calls=%fused_computation.14 | convolution fusion | flops 2944860160 | bytes 14778368 | tf_op jit(solution)/shard_map/td,fd->tf/dot_general | solution.py:561
  337.5 1.8 collective-permute-start.1
  339.3 0.5 collective-permute-start.2
  339.7 4.1 add_convert_fusion
  343.9 0.0 copy-start.23
  343.9 0.0 copy-start.13
  344.0 10.3 %fusion.7 = bf16[2048,1376]{0,1:T(8,128)(2,1)} fusion(bf16[2048,1376]{0,1:T(8,128)(2,1)S(1)} %bitcast.78, bf16[2048,512]{1,0:T(8,128)(2,1)S(1)} %add_convert_fusion, bf16[2,1376,512]{2,1,0:T(8,128)(2,1)S(1)} %copy-done.9), kind=kOutput, calls=%fused_computation.17 | convolution fusion | flops 2944860160 | bytes 14778368 | tf_op jit(solution)/shard_map/td,fd->tf/dot_general | solution.py:561
  354.3 0.0 collective-permute-start.5
  354.3 0.5 collective-permute-start.6
  354.8 9.1 %fusion.27.down_0 = f32[1376,128]{1,0:T(8,128)} fusion(bf16[2048,512]{1,0:T(8,128)(2,1)} %copy-done.23, bf16[2,512,128]{2,1,0:T(8,128)(2,1)S(1)} %copy-done.13, bf16[2048,1376]{0,1:T(8,128)(2,1)} %copy-done.20), kind=kOutput, calls=%fused_computation.42 | convolution fusion | flops 3094216704 | bytes 8568832 | tf_op jit(solution)/shard_map/dot_general | solution.py:574
  363.9 6.9 %fusion.30.up_0 = f32[1376,128]{1,0:T(8,128)S(1)} fusion(bf16[2048,1376]{0,1:T(8,128)(2,1)} %fusion.7, bf16[2048,512]{1,0:T(8,128)(2,1)} %param.13, bf16[2,512,128]{2,1,0:T(8,128)(2,1)S(1)} %copy-done.11), kind=kOutput, calls=%fused_computation.44 | convolution fusion | flops 3066036224 | bytes 8568832 | tf_op jit(solution)/shard_map/dot_general | solution.py:573
  370.8 14.7 %collective-permute-done.1.refs_0_ = bf16[512,2048]{1,0:T(8,128)(2,1)S(1)} collective-permute-done((bf16[512,2048]{1,0:T(8,128)(2,1)}, bf16[512,2048]{1,0:T(8,128)(2,1)S(1)}, u32[]{:S(2)}, u32[]{:S(2)}) %collective-permute-start.1) | collective-permute-done | bytes 2097184 | tf_op jit(solution)/shard_map/ppermute | solution.py:362
  385.4 1.6 collective-permute-done.2.refs_1_
  387.0 0.0 collective-permute-start.3
  387.0 0.5 collective-permute-start.4
  387.5 0.4 collective-permute-start.7
  388.0 0.0 collective-permute-done.5.refs_2_
  388.0 0.3 collective-permute-start.8
  388.4 0.9 copy.26
  389.3 0.9 copy.28
  390.3 0.1 pad_maximum_fusion.1
  390.3 0.0 collective-permute-done.6.refs_3_
  390.3 22.3 %place.4 = (bf16[512,32000]{1,0:T(8,128)(2,1)}, f32[4000,512]{1,0:T(8,128)}, f32[4000,512]{1,0:T(8,128)}) custom-call(bf16[512,2048]{1,0:T(8,128)(2,1)} %get-tuple-element.42.refs_0_, bf16[512,2048]{1,0:T(8,128)(2,1)} %get-tuple-element.43.refs_1_, bf16[512,2048]{1,0:T(8,128)(2,1)} %collective-permute-done.5.refs_2_, ...), custom_call_target="tpu_custom_call" | custom-call | flops 6000000000 | bytes 16777216 | tf_op jit(solution)/shard_map/place/pallas_call | solution.py:434
  412.6 0.0 collective-permute-done.3.refs_2_
  412.6 4.8 place.5.refs_4_
  417.4 18.0 %collective-permute-done.7.refs_0_ = bf16[512,2048]{1,0:T(8,128)(2,1)} collective-permute-done((bf16[512,2048]{1,0:T(8,128)(2,1)}, bf16[512,2048]{1,0:T(8,128)(2,1)}, u32[]{:S(2)}, u32[]{:S(2)}) %collective-permute-start.7) | collective-permute-done | bytes 2097184 | tf_op jit(solution)/shard_map/ppermute | solution.py:362
  435.4 0.2 collective-permute-done.8.refs_1_
  435.6 0.5 collective-permute-start.10
  436.1 7.7 %fusion.24.up_1 = f32[1376,128]{1,0:T(8,128)} fusion(bf16[2048,1376]{0,1:T(8,128)(2,1)} %copy-done.21, bf16[2048,512]{1,0:T(8,128)(2,1)} %copy-done.22, bf16[2,512,128]{2,1,0:T(8,128)(2,1)} %param.18), kind=kOutput, calls=%fused_computation.40 | convolution fusion | flops 3066036224 | bytes 8568832 | tf_op jit(solution)/shard_map/dot_general | solution.py:573
  443.7 9.1 %fusion.21.down_1 = f32[1376,128]{1,0:T(8,128)} fusion(bf16[2048,512]{1,0:T(8,128)(2,1)} %copy-done, bf16[2,512,128]{2,1,0:T(8,128)(2,1)} %param.19, bf16[2048,1376]{0,1:T(8,128)(2,1)} %copy-done.19), kind=kOutput, calls=%fused_computation.38 | convolution fusion | flops 3094216704 | bytes 8568832 | tf_op jit(solution)/shard_map/dot_general | solution.py:574
  452.8 1.6 collective-permute-start.11
  454.4 0.3 collective-permute-start.12
  454.7 6.4 %place.6.refs_4_ = bf16[512,32000]{1,0:T(8,128)(2,1)} custom-call(bf16[512,2048]{1,0:T(8,128)(2,1)} %collective-permute-done.7.refs_0_, bf16[512,2048]{1,0:T(8,128)(2,1)} %collective-permute-done.8.refs_1_, bf16[512,2048]{1,0:T(8,128)(2,1)} %collective-permute-done.9.refs_2_, ...), custom_call_target="tpu_custom_call", output_to_operand_aliasing={{}: (4, {})} | custom-call | flops 3000000000 | bytes 16777216 | tf_op jit(solution)/shard_map/place/pallas_call | solution.py:434
  461.2 0.0 copy-start.6
  461.2 0.0 copy-start.12
  461.2 66.8 %small_update.1 = (f32[4,172,128]{2,1,0:T(8,128)S(1)}, f32[4,172,128]{2,1,0:T(8,128)S(1)}, bf16[2,1376,128]{2,1,0:T(8,128)(2,1)S(1)}, bf16[2,1376,128]{2,1,0:T(8,128)(2,1)S(1)}) custom-call(f32[1376,128]{1,0:T(8,128)S(1)} %fusion.30.up_0, f32[1376,128]{1,0:T(8,128)S(1)} %copy-done.1, f32[1376,128]{1,0:T(8,128)S(1)} %copy-done.2, f32[1376,128]{1,0:T(8,128)S(1)} %copy-done.3, ...), custom_call_target="tpu_custom_call" | custom-call | flops 30000001024 | bytes 10000000 | tf_op jit(solution)/shard_map/small_update/pallas_call | solution.py:520
  528.0 0.0 copy-start.10
  528.0 0.0 copy-start.14
  528.0 0.0 collective-permute-done.11.refs_0_
  528.1 0.0 collective-permute-done.12.refs_1_
  528.1 0.4 collective-permute-start.13
  528.5 0.1 collective-permute-start.14
  528.6 0.8 copy.31
  529.4 0.8 copy.29
  530.2 0.8 copy.32
  530.9 0.8 copy.30
  531.7 2.5 fusion.20
  534.2 2.4 subtract_convert_fusion
  536.6 4.0 place.7
  (51 shorter events, 0.2 us)
Async XLA Ops:
  1.7 9.2 %copy-start.7 = (bf16[2,1376,512]{2,1,0:T(8,128)(2,1)S(1)}, bf16[2,1376,512]{2,1,0:T(8,128)(2,1)}, u32[]{:S(2)}) copy-start(bf16[2,1376,512]{2,1,0:T(8,128)(2,1)} %param.16) | copy-start | bytes 8454148
  1.7 9.2 %copy-start.17 = (bf16[2048,512]{1,0:T(8,128)(2,1)S(1)}, bf16[2048,512]{1,0:T(8,128)(2,1)}, u32[]{:S(2)}) copy-start(bf16[2048,512]{1,0:T(8,128)(2,1)} %param.13) | copy-start | bytes 6291460
  1.8 24.6 %collective-permute-start = (f32[2,96,512]{2,1,0:T(8,128)S(1)}, f32[2,96,512]{2,1,0:T(8,128)S(1)}, u32[]{:S(2)}, u32[]{:S(2)}) collective-permute-start(f32[2,96,512]{2,1,0:T(8,128)S(1)} %pad_maximum_fusion), channel_id=1, source_target_pairs={{1,0},{2,1},{3,2},{4,3},{5,4},{6,5},{7,6}} | collective-permute-start | bytes 1179656 | tf_op jit(solution)/shard_map/ppermute | solution.py:547
  8.4 2.5 copy-start.20
  10.9 5.8 %copy-start.4 = (bf16[2,512,1376]{1,2,0:T(8,128)(2,1)S(1)}, bf16[2,512,1376]{1,2,0:T(8,128)(2,1)}, u32[]{:S(2)}) copy-start(bf16[2,512,1376]{1,2,0:T(8,128)(2,1)} %param.15) | copy-start | bytes 8454148
  16.7 3.4 copy-start.22
  20.1 6.3 %copy-start.19 = (bf16[2048,1376]{0,1:T(8,128)(2,1)}, bf16[2048,1376]{0,1:T(8,128)(2,1)S(1)}, u32[]{:S(2)}) copy-start(bf16[2048,1376]{0,1:T(8,128)(2,1)S(1)} %convolution_convert_fusion) | copy-start | bytes 16908292
  26.4 0.7 copy-start.18
  27.1 299.0 %copy-start.8 = (bf16[2,1376,512]{2,1,0:T(8,128)(2,1)S(1)}, bf16[2,1376,512]{2,1,0:T(8,128)(2,1)}, u32[]{:S(2)}) copy-start(bf16[2,1376,512]{2,1,0:T(8,128)(2,1)} %param.16) | copy-start | bytes 8454148
  326.1 13.7 %copy-start = (bf16[2048,512]{1,0:T(8,128)(2,1)}, bf16[2048,512]{1,0:T(8,128)(2,1)S(1)}, u32[]{:S(2)}) copy-start(bf16[2048,512]{1,0:T(8,128)(2,1)S(1)} %get-tuple-element.36) | copy-start | bytes 6291460
  326.1 13.7 %copy-start.5 = (bf16[2,512,1376]{1,2,0:T(8,128)(2,1)S(1)}, bf16[2,512,1376]{1,2,0:T(8,128)(2,1)}, u32[]{:S(2)}) copy-start(bf16[2,512,1376]{1,2,0:T(8,128)(2,1)} %param.15) | copy-start | bytes 8454148
  337.5 6.4 %copy-start.21 = (bf16[2048,1376]{0,1:T(8,128)(2,1)}, bf16[2048,1376]{0,1:T(8,128)(2,1)S(1)}, u32[]{:S(2)}) copy-start(bf16[2048,1376]{0,1:T(8,128)(2,1)S(1)} %fusion.4) | copy-start | bytes 16908292
  337.5 47.9 %collective-permute-start.1 = (bf16[512,2048]{1,0:T(8,128)(2,1)}, bf16[512,2048]{1,0:T(8,128)(2,1)S(1)}, u32[]{:S(2)}, u32[]{:S(2)}) collective-permute-start(bf16[512,2048]{1,0:T(8,128)(2,1)} %get-tuple-element.42.refs_0_), channel_id=1, source_target_pairs={{0,2},{1,3},{2,0},{3,1},{4,6},{5,7},{6,4},{7,5}} | collective-permute-start | bytes 6291464 | tf_op jit(solution)/shard_map/ppermute | solution.py:362
  339.3 4.6 slice-start
  339.3 4.6 copy-start.9
  339.3 4.7 slice-start.1
  339.3 47.8 %collective-permute-start.2 = (bf16[512,2048]{1,0:T(8,128)(2,1)}, bf16[512,2048]{1,0:T(8,128)(2,1)}, u32[]{:S(2)}, u32[]{:S(2)}) collective-permute-start(bf16[512,2048]{1,0:T(8,128)(2,1)} %get-tuple-element.43.refs_1_), channel_id=1, source_target_pairs={{0,4},{1,5},{2,6},{3,7},{4,0},{5,1},{6,2},{7,3}} | collective-permute-start | bytes 6291464 | tf_op jit(solution)/shard_map/ppermute | solution.py:362
  343.9 10.4 %copy-start.23 = (bf16[2048,512]{1,0:T(8,128)(2,1)}, bf16[2048,512]{1,0:T(8,128)(2,1)S(1)}, u32[]{:S(2)}) copy-start(bf16[2048,512]{1,0:T(8,128)(2,1)S(1)} %add_convert_fusion) | copy-start | bytes 6291460
  343.9 10.9 %copy-start.13 = (bf16[2,512,128]{2,1,0:T(8,128)(2,1)S(1)}, bf16[2,512,128]{2,1,0:T(8,128)(2,1)}, u32[]{:S(2)}) copy-start(bf16[2,512,128]{2,1,0:T(8,128)(2,1)} %param.19) | copy-start | bytes 786436
  354.3 9.6 %copy-start.11 = (bf16[2,512,128]{2,1,0:T(8,128)(2,1)S(1)}, bf16[2,512,128]{2,1,0:T(8,128)(2,1)}, u32[]{:S(2)}) copy-start(bf16[2,512,128]{2,1,0:T(8,128)(2,1)} %param.18) | copy-start | bytes 786436
  354.3 33.7 %collective-permute-start.5 = (bf16[512,2048]{1,0:T(8,128)(2,1)}, bf16[512,2048]{1,0:T(8,128)(2,1)}, u32[]{:S(2)}, u32[]{:S(2)}) collective-permute-start(bf16[512,2048]{1,0:T(8,128)(2,1)} %get-tuple-element.42.refs_0_), channel_id=1, source_target_pairs={{0,1},{1,0},{2,3},{3,2},{4,5},{5,4},{6,7},{7,6}} | collective-permute-start | bytes 6291464 | tf_op jit(solution)/shard_map/ppermute | solution.py:362
  354.3 36.0 %collective-permute-start.6 = (bf16[512,2048]{1,0:T(8,128)(2,1)}, bf16[512,2048]{1,0:T(8,128)(2,1)}, u32[]{:S(2)}, u32[]{:S(2)}) collective-permute-start(bf16[512,2048]{1,0:T(8,128)(2,1)} %get-tuple-element.43.refs_1_), channel_id=1, source_target_pairs={{0,1},{1,0},{2,3},{3,2},{4,5},{5,4},{6,7},{7,6}} | collective-permute-start | bytes 6291464 | tf_op jit(solution)/shard_map/ppermute | solution.py:362
  363.9 24.4 %copy-start.15 = (f32[2,128,172]{1,0,2:T(2,128)S(1)}, f32[2,128,172]{1,0,2:T(2,128)}, u32[]{:S(2)}) copy-start(f32[2,128,172]{1,0,2:T(2,128)} %param.20) | copy-start | bytes 528388
  363.9 24.4 %copy-start.16 = (f32[2,128,172]{1,0,2:T(2,128)S(1)}, f32[2,128,172]{1,0,2:T(2,128)}, u32[]{:S(2)}) copy-start(f32[2,128,172]{1,0,2:T(2,128)} %param.21) | copy-start | bytes 528388
  387.0 25.6 %collective-permute-start.3 = (bf16[512,2048]{1,0:T(8,128)(2,1)S(1)}, bf16[512,2048]{1,0:T(8,128)(2,1)S(1)}, u32[]{:S(2)}, u32[]{:S(2)}) collective-permute-start(bf16[512,2048]{1,0:T(8,128)(2,1)S(1)} %collective-permute-done.1.refs_0_), channel_id=1, source_target_pairs={{0,1},{1,0},{2,3},{3,2},{4,5},{5,4},{6,7},{7,6}} | collective-permute-start | bytes 6291464 | tf_op jit(solution)/shard_map/ppermute | solution.py:362
  387.0 25.6 %collective-permute-start.4 = (bf16[512,2048]{1,0:T(8,128)(2,1)}, bf16[512,2048]{1,0:T(8,128)(2,1)S(1)}, u32[]{:S(2)}, u32[]{:S(2)}) collective-permute-start(bf16[512,2048]{1,0:T(8,128)(2,1)} %collective-permute-done.2.refs_1_), channel_id=1, source_target_pairs={{0,1},{1,0},{2,3},{3,2},{4,5},{5,4},{6,7},{7,6}} | collective-permute-start | bytes 6291464 | tf_op jit(solution)/shard_map/ppermute | solution.py:362
  387.5 47.9 %collective-permute-start.7 = (bf16[512,2048]{1,0:T(8,128)(2,1)}, bf16[512,2048]{1,0:T(8,128)(2,1)}, u32[]{:S(2)}, u32[]{:S(2)}) collective-permute-start(bf16[512,2048]{1,0:T(8,128)(2,1)} %get-tuple-element.42.refs_0_), channel_id=1, source_target_pairs={{0,4},{1,5},{2,6},{3,7},{4,0},{5,1},{6,2},{7,3}} | collective-permute-start | bytes 6291464 | tf_op jit(solution)/shard_map/ppermute | solution.py:362
  388.0 47.6 %collective-permute-start.8 = (bf16[512,2048]{1,0:T(8,128)(2,1)}, bf16[512,2048]{1,0:T(8,128)(2,1)}, u32[]{:S(2)}, u32[]{:S(2)}) collective-permute-start(bf16[512,2048]{1,0:T(8,128)(2,1)} %get-tuple-element.43.refs_1_), channel_id=1, source_target_pairs={{0,2},{1,3},{2,0},{3,1},{4,6},{5,7},{6,4},{7,5}} | collective-permute-start | bytes 6291464 | tf_op jit(solution)/shard_map/ppermute | solution.py:362
  435.6 19.2 %collective-permute-start.9 = (bf16[512,2048]{1,0:T(8,128)(2,1)}, bf16[512,2048]{1,0:T(8,128)(2,1)}, u32[]{:S(2)}, u32[]{:S(2)}) collective-permute-start(bf16[512,2048]{1,0:T(8,128)(2,1)} %collective-permute-done.7.refs_0_), channel_id=1, source_target_pairs={{0,1},{1,0},{2,3},{3,2},{4,5},{5,4},{6,7},{7,6}} | collective-permute-start | bytes 6291464 | tf_op jit(solution)/shard_map/ppermute | solution.py:362
  435.6 19.2 %collective-permute-start.10 = (bf16[512,2048]{1,0:T(8,128)(2,1)}, bf16[512,2048]{1,0:T(8,128)(2,1)}, u32[]{:S(2)}, u32[]{:S(2)}) collective-permute-start(bf16[512,2048]{1,0:T(8,128)(2,1)} %collective-permute-done.8.refs_1_), channel_id=1, source_target_pairs={{0,1},{1,0},{2,3},{3,2},{4,5},{5,4},{6,7},{7,6}} | collective-permute-start | bytes 6291464 | tf_op jit(solution)/shard_map/ppermute | solution.py:362
  452.8 8.4 %copy-start.1 = (f32[1376,128]{1,0:T(8,128)S(1)}, f32[1376,128]{1,0:T(8,128)}, u32[]{:S(2)}) copy-start(f32[1376,128]{1,0:T(8,128)} %fusion.24.up_1) | copy-start | bytes 2113540
  452.8 8.4 %copy-start.2 = (f32[1376,128]{1,0:T(8,128)S(1)}, f32[1376,128]{1,0:T(8,128)}, u32[]{:S(2)}) copy-start(f32[1376,128]{1,0:T(8,128)} %fusion.27.down_0) | copy-start | bytes 2113540
  452.8 8.4 %copy-start.3 = (f32[1376,128]{1,0:T(8,128)S(1)}, f32[1376,128]{1,0:T(8,128)}, u32[]{:S(2)}) copy-start(f32[1376,128]{1,0:T(8,128)} %fusion.21.down_1) | copy-start | bytes 2113540
  452.8 75.2 %collective-permute-start.11 = (bf16[512,2048]{1,0:T(8,128)(2,1)S(1)}, bf16[512,2048]{1,0:T(8,128)(2,1)S(1)}, u32[]{:S(2)}, u32[]{:S(2)}) collective-permute-start(bf16[512,2048]{1,0:T(8,128)(2,1)S(1)} %collective-permute-done.1.refs_0_), channel_id=1, source_target_pairs={{0,4},{1,5},{2,6},{3,7},{4,0},{5,1},{6,2},{7,3}} | collective-permute-start | bytes 6291464 | tf_op jit(solution)/shard_map/ppermute | solution.py:362
  454.4 73.7 %collective-permute-start.12 = (bf16[512,2048]{1,0:T(8,128)(2,1)}, bf16[512,2048]{1,0:T(8,128)(2,1)S(1)}, u32[]{:S(2)}, u32[]{:S(2)}) collective-permute-start(bf16[512,2048]{1,0:T(8,128)(2,1)} %collective-permute-done.2.refs_1_), channel_id=1, source_target_pairs={{0,2},{1,3},{2,0},{3,1},{4,6},{5,7},{6,4},{7,5}} | collective-permute-start | bytes 6291464 | tf_op jit(solution)/shard_map/ppermute | solution.py:362
  461.2 70.5 %copy-start.6 = (bf16[2,512,1376]{1,2,0:T(8,128)(2,1)S(1)}, bf16[2,512,1376]{1,2,0:T(8,128)(2,1)}, u32[]{:S(2)}) copy-start(bf16[2,512,1376]{1,2,0:T(8,128)(2,1)} %param.15) | copy-start | bytes 8454148
  461.2 70.5 %copy-start.12 = (bf16[2,512,128]{2,1,0:T(8,128)(2,1)S(1)}, bf16[2,512,128]{2,1,0:T(8,128)(2,1)}, u32[]{:S(2)}) copy-start(bf16[2,512,128]{2,1,0:T(8,128)(2,1)} %param.18) | copy-start | bytes 786436
  528.0 6.1 %copy-start.10 = (bf16[2,1376,512]{2,1,0:T(8,128)(2,1)S(1)}, bf16[2,1376,512]{2,1,0:T(8,128)(2,1)}, u32[]{:S(2)}) copy-start(bf16[2,1376,512]{2,1,0:T(8,128)(2,1)} %param.16) | copy-start | bytes 8454148
  528.0 6.1 %copy-start.14 = (bf16[2,512,128]{2,1,0:T(8,128)(2,1)S(1)}, bf16[2,512,128]{2,1,0:T(8,128)(2,1)}, u32[]{:S(2)}) copy-start(bf16[2,512,128]{2,1,0:T(8,128)(2,1)} %param.19) | copy-start | bytes 786436
  528.1 8.6 %collective-permute-start.13 = (bf16[512,2048]{1,0:T(8,128)(2,1)S(1)}, bf16[512,2048]{1,0:T(8,128)(2,1)S(1)}, u32[]{:S(2)}, u32[]{:S(2)}) collective-permute-start(bf16[512,2048]{1,0:T(8,128)(2,1)S(1)} %collective-permute-done.11.refs_0_), channel_id=1, source_target_pairs={{0,1},{1,0},{2,3},{3,2},{4,5},{5,4},{6,7},{7,6}} | collective-permute-start | bytes 6291464 | tf_op jit(solution)/shard_map/ppermute | solution.py:362
  528.5 8.2 %collective-permute-start.14 = (bf16[512,2048]{1,0:T(8,128)(2,1)S(1)}, bf16[512,2048]{1,0:T(8,128)(2,1)S(1)}, u32[]{:S(2)}, u32[]{:S(2)}) collective-permute-start(bf16[512,2048]{1,0:T(8,128)(2,1)S(1)} %collective-permute-done.12.refs_1_), channel_id=1, source_target_pairs={{0,1},{1,0},{2,3},{3,2},{4,5},{5,4},{6,7},{7,6}} | collective-permute-start | bytes 6291464 | tf_op jit(solution)/shard_map/ppermute | solution.py:362

commit v2 on v1

--- a/solution.py
+++ b/solution.py
@@ -21,7 +21,7 @@
 BLK = 512
 SUBS = 8
 SHARD = 4000
-RING = 6
+RING = 5
 EDGE = 96
 DRING = 4
 
@@ -29,6 +29,8 @@
 GROUP_PAIR = (0, 0, 1, 1, 0, 2, 2, 1, 0, 3, 3, 2, 1, 3, 2, 3)
 GROUP_SEND = (0, 1, 2, 3, 4, 5, 6, 7, 0, 8, 9, 10, 0, 11, 0, 0)
 BLOCKS = 64
+LAG = 2
+SLOTS = LAG + 2
 
 
 def lookup(index, values):
@@ -80,7 +82,7 @@
 
     def fetch(n):
         col = decode(n)[-1]
-        slot = lax.rem(n, 2)
+        slot = lax.rem(n, SLOTS)
         return (pltpu.make_async_copy(d_logits.at[:, pl.ds(col, BLK)], dz_buf.at[slot], dz_sem.at[slot]),
                 pltpu.make_async_copy(w_out.at[:, pl.ds(col, BLK)], wo_buf.at[slot], wo_sem.at[slot]))
 
@@ -157,8 +159,8 @@
 
 
     def body(n, carry):
-        group, half, own, rel, sub, dest, col = decode(n)
-        slot = lax.rem(n, 2)
+        group, half, own, rel, sub, _, _ = decode(n)
+        slot = lax.rem(n, SLOTS)
 
         @pl.when(n + 1 < BLOCKS)
         def _():
@@ -245,15 +247,23 @@
             stage[place] = acc[half] + add_core[half] + add_first[half]
             to_second(place, sub, device).start()
 
-        lane = lax.broadcasted_iota(jnp.int32, (1, BLK), 1) + (col - SHARD * dest)
-        keep = jnp.where(jnp.logical_and(lane >= 0, lane < SHARD), 1.0, 0.0).astype(jnp.bfloat16)
-        weights = wo_buf[slot] * keep
-
-        @pl.loop(0, 4)
-        def _(tile):
-            rows = pl.ds(pl.multiple_of(tile * 512, 512), 512)
-            g_acc[rows, :] += lax.dot_general(dz_buf[slot, rows, :], weights, (((1,), (1,)), ((), ())),
-                                              preferred_element_type=jnp.float32)
+        def hidden_part(block, carry):
+            _, _, _, _, _, dest, col = decode(block)
+            slot = lax.rem(block, SLOTS)
+            lane = lax.broadcasted_iota(jnp.int32, (1, BLK), 1) + (col - SHARD * dest)
+            keep = jnp.where(jnp.logical_and(lane >= 0, lane < SHARD), 1.0, 0.0).astype(jnp.bfloat16)
+            weights = wo_buf[slot] * keep
+
+            @pl.loop(0, 4)
+            def _(tile):
+                rows = pl.ds(pl.multiple_of(tile * 512, 512), 512)
+                g_acc[rows, :] += lax.dot_general(dz_buf[slot, rows, :], weights, (((1,), (1,)), ((), ())),
+                                                  preferred_element_type=jnp.float32)
+
+            return carry
+
+        last = n == BLOCKS - 1
+        lax.fori_loop(jnp.maximum(n - LAG, 0), jnp.where(last, BLOCKS, jnp.maximum(n - LAG + 1, 0)), hidden_part, 0)
 
         @pl.when(jnp.logical_and(is_final, half == 1))
         def _():
@@ -321,8 +331,8 @@
         out_specs=(any_spec, any_spec, any_spec, any_spec, vmem, any_spec, any_spec),
         scratch_shapes=[
             pltpu.VMEM((dim, tokens), bf16),
-            pltpu.VMEM((2, tokens, BLK), bf16),
-            pltpu.VMEM((2, dim, BLK), bf16),
+            pltpu.VMEM((SLOTS, tokens, BLK), bf16),
+            pltpu.VMEM((SLOTS, dim, BLK), bf16),
             pltpu.VMEM((2, dim, BLK), f32),
             pltpu.VMEM((tokens, dim), f32),
             pltpu.VMEM((2, dim, BLK), f32),
@@ -331,8 +341,8 @@
             pltpu.VMEM((2 * RING + DRING, dim, BLK), f32),
             pltpu.VMEM((2, 2, BLK + 2 * EDGE, dim), f32),
             pltpu.VMEM((2, dim, BLK), bf16),
-            pltpu.SemaphoreType.DMA((2,)),
-            pltpu.SemaphoreType.DMA((2,)),
+            pltpu.SemaphoreType.DMA((SLOTS,)),
+            pltpu.SemaphoreType.DMA((SLOTS,)),
             pltpu.SemaphoreType.DMA((4 * SUBS,)),
             pltpu.SemaphoreType.DMA((2 * SUBS,)),
             pltpu.SemaphoreType.DMA((SUBS,)),
@@ -343,7 +353,7 @@
             pltpu.SemaphoreType.DMA((2, 2, 7)),
             pltpu.SemaphoreType.DMA((2,)),
         ],
-        compiler_params=pltpu.CompilerParams(collective_id=0, has_side_effects=True, vmem_limit_bytes=56 * 1024 * 1024),
+        compiler_params=pltpu.CompilerParams(collective_id=0, has_side_effects=True, vmem_limit_bytes=58 * 1024 * 1024),
         cost_estimate=pl.CostEstimate(flops=280_000_000_000, bytes_accessed=300_000_000, transcendentals=0),
         name='head_update',
     )(hidden, d_logits, w_out, mom_t, var_t, edge)

time: 544 us -> 540 us (level)
  transfers between devices with their start and end apart: 15 -> 15, of which waited for: 4 -> 3; matrix products, arithmetic and copies ran while one was open for 14% -> 14% of each run, Pallas kernels for 19% -> 19%
where the time goes in v2:
time: 540 us; the launch traced here: 537 us
  Pallas kernels  400 us (74%)
  matrix products  83.9 us (16%)
  waiting for transfers between devices  33.5 us (6%)
  local copies, waits for them, and re-layouts  9.39 us (2%)
  starting transfers between devices  9.16 us (2%)
    pallas_call x1, Pallas kernels, head_update(): pl.pallas_call(head_kernel, out_shape=(jax.ShapeDtypeStruct((dim, SUBS *...  296 us
    pallas_call x1, Pallas kernels, small_update(): pl.pallas_call(small_kernel, out_shape=(jax.ShapeDtypeStruct(shape, f32),...  66.3 us
    pallas_call x4, Pallas kernels, place(): pl.pallas_call(functools.partial(place_kernel, origins, len(copies), int(...  37.4 us
    ppermute x14, waiting for transfers between devices, permute(): lax.ppermute(value, DATA_AXIS, [(dev, dev ^ mask) for dev in range(8)])  33.5 us
    dot_general x2, matrix products, local_step(): jnp.einsum('td,fd->tf', grad_hidden, w_down[layer_idx], preferred_element...  21.7 us
    dot_general x2, matrix products, local_step(): jnp.dot(grad_down, proj_down[layer_idx].astype(jnp.float32), preferred_el...  18.2 us
    dot_general x2, matrix products, local_step(): jnp.dot(grad_up, proj_up[layer_idx].astype(jnp.float32), preferred_elemen...  14.5 us
    dot_general x2, matrix products, local_step(): jnp.dot(post_act, w_down[layer_idx], preferred_element_type=jnp.float32)  12 us
  transfers between devices with their start and end apart: 15, of which 3 were waited for; matrix products, arithmetic and copies ran while one was open for 14% of the time, Pallas kernels for 19%

profile of v2, /device:TPU:0, one launch (start us, length us, event | category | flops | bytes accessed | tf_op | source)
XLA Modules:
  0.0 537.0 jit_solution(4411400600134722957)
XLA Ops:
  0.6 1.1 slice_bitcast_fusion
  1.7 0.0 copy-start.7
  1.7 0.0 copy-start.17
  1.8 1.6 collective-permute-start
  3.3 5.1 convolution_convert_fusion.1
  8.4 0.0 copy-start.20
  8.4 2.5 copy-done.20
  10.9 5.8 %add_convert_fusion.2 = bf16[2048,512]{1,0:T(8,128)(2,1)S(1)} fusion(bf16[2048,512]{1,0:T(8,128)(2,1)S(1)} %copy-done.17, bf16[2,1376,512]{2,1,0:T(8,128)(2,1)S(1)} %copy-done.7, bf16[2048,1376]{0,1:T(8,128)(2,1)S(1)} %convolution_convert_fusion.1), kind=kOutput, calls=%fused_computation.37 | convolution fusion | flops 2917007360 | bytes 11239424 | tf_op jit(solution)/shard_map/dot_general | solution.py:553
  16.7 0.0 copy-start.22
  16.7 3.3 convolution_convert_fusion
  20.1 6.3 %add_convert_fusion.1.hidden = bf16[2048,512]{1,0:T(8,128)(2,1)} fusion(bf16[2048,512]{1,0:T(8,128)(2,1)S(1)} %add_convert_fusion.2, bf16[2,1376,512]{2,1,0:T(8,128)(2,1)S(1)} %copy-done.7, bf16[2048,1376]{0,1:T(8,128)(2,1)S(1)} %convolution_convert_fusion), kind=kOutput, calls=%fused_computation.36 | convolution fusion | flops 2917007360 | bytes 11239424 | tf_op jit(solution)/shard_map/dot_general | solution.py:553
  26.4 0.0 collective-permute-done.edge
  26.4 0.7 copy-done.18
  27.1 296.0 %head_update.1 = (bf16[512,2048]{1,0:T(8,128)(2,1)}, bf16[512,2048]{1,0:T(8,128)(2,1)}, f32[4000,512]{1,0:T(8,128)}, f32[4000,512]{1,0:T(8,128)}, bf16[2048,512]...) custom-call(bf16[2048,512]{1,0:T(8,128)(2,1)} %add_convert_fusion.1.hidden, ...), custom_call_target="tpu_custom_call" | custom-call | flops 280000004096 | bytes 300000000 | tf_op jit(solution)/shard_map/head_update/pallas_call | solution.py:319
  323.1 0.0 copy-start.5
  323.1 11.4 %fusion.4 = bf16[2048,1376]{0,1:T(8,128)(2,1)S(1)} fusion(bf16[2048,1376]{0,1:T(8,128)(2,1)} %copy-done.19, bf16[2048,512]{1,0:T(8,128)(2,1)S(1)} %get-tuple-element.36, bf16[2,1376,512]{2,1,0:T(8,128)(2,1)S(1)} %copy-done.8), kind=kOutput, calls=%fused_computation.14 | convolution fusion | flops 2944860160 | bytes 14778368 | tf_op jit(solution)/shard_map/td,fd->tf/dot_general | solution.py:571
  334.5 1.1 collective-permute-start.1
  335.6 0.5 collective-permute-start.2
  336.1 4.1 add_convert_fusion
  340.3 0.0 copy-start.23
  340.3 0.0 copy-start.13
  340.3 10.3 %fusion.7 = bf16[2048,1376]{0,1:T(8,128)(2,1)} fusion(bf16[2048,1376]{0,1:T(8,128)(2,1)S(1)} %bitcast.78, bf16[2048,512]{1,0:T(8,128)(2,1)S(1)} %add_convert_fusion, bf16[2,1376,512]{2,1,0:T(8,128)(2,1)S(1)} %copy-done.9), kind=kOutput, calls=%fused_computation.17 | convolution fusion | flops 2944860160 | bytes 14778368 | tf_op jit(solution)/shard_map/td,fd->tf/dot_general | solution.py:571
  350.6 0.0 collective-permute-start.5
  350.6 0.5 collective-permute-start.6
  351.2 9.1 %fusion.27.down_0 = f32[1376,128]{1,0:T(8,128)} fusion(bf16[2048,512]{1,0:T(8,128)(2,1)} %copy-done.23, bf16[2,512,128]{2,1,0:T(8,128)(2,1)S(1)} %copy-done.13, bf16[2048,1376]{0,1:T(8,128)(2,1)} %copy-done.20), kind=kOutput, calls=%fused_computation.42 | convolution fusion | flops 3094216704 | bytes 8568832 | tf_op jit(solution)/shard_map/dot_general | solution.py:584
  360.2 6.9 %fusion.30.up_0 = f32[1376,128]{1,0:T(8,128)S(1)} fusion(bf16[2048,1376]{0,1:T(8,128)(2,1)} %fusion.7, bf16[2048,512]{1,0:T(8,128)(2,1)} %param.13, bf16[2,512,128]{2,1,0:T(8,128)(2,1)S(1)} %copy-done.11), kind=kOutput, calls=%fused_computation.44 | convolution fusion | flops 3066036224 | bytes 8568832 | tf_op jit(solution)/shard_map/dot_general | solution.py:583
  367.1 15.0 %collective-permute-done.1.refs_0_ = bf16[512,2048]{1,0:T(8,128)(2,1)S(1)} collective-permute-done((bf16[512,2048]{1,0:T(8,128)(2,1)}, bf16[512,2048]{1,0:T(8,128)(2,1)S(1)}, u32[]{:S(2)}, u32[]{:S(2)}) %collective-permute-start.1) | collective-permute-done | bytes 2097184 | tf_op jit(solution)/shard_map/ppermute | solution.py:372
  382.1 0.9 collective-permute-done.2.refs_1_
  383.0 0.5 collective-permute-start.4
  383.5 0.3 collective-permute-start.7
  383.8 0.0 collective-permute-done.5.refs_2_
  383.8 1.0 collective-permute-start.8
  384.9 0.9 copy.26
  385.8 0.9 copy.28
  386.7 0.1 pad_maximum_fusion.1
  386.8 0.0 collective-permute-done.6.refs_3_
  386.8 22.3 %place.4 = (bf16[512,32000]{1,0:T(8,128)(2,1)}, f32[4000,512]{1,0:T(8,128)}, f32[4000,512]{1,0:T(8,128)}) custom-call(bf16[512,2048]{1,0:T(8,128)(2,1)} %get-tuple-element.42.refs_0_, bf16[512,2048]{1,0:T(8,128)(2,1)} %get-tuple-element.43.refs_1_, bf16[512,2048]{1,0:T(8,128)(2,1)} %collective-permute-done.5.refs_2_, ...), custom_call_target="tpu_custom_call" | custom-call | flops 6000000000 | bytes 16777216 | tf_op jit(solution)/shard_map/place/pallas_call | solution.py:444
  409.1 0.0 collective-permute-done.3.refs_2_
  409.1 4.8 place.5.refs_4_
  413.9 17.5 %collective-permute-done.7.refs_0_ = bf16[512,2048]{1,0:T(8,128)(2,1)} collective-permute-done((bf16[512,2048]{1,0:T(8,128)(2,1)}, bf16[512,2048]{1,0:T(8,128)(2,1)}, u32[]{:S(2)}, u32[]{:S(2)}) %collective-permute-start.7) | collective-permute-done | bytes 2097184 | tf_op jit(solution)/shard_map/ppermute | solution.py:372
  431.4 0.0 collective-permute-done.8.refs_1_
  431.4 0.5 collective-permute-start.10
  431.9 7.7 %fusion.24.up_1 = f32[1376,128]{1,0:T(8,128)} fusion(bf16[2048,1376]{0,1:T(8,128)(2,1)} %copy-done.21, bf16[2048,512]{1,0:T(8,128)(2,1)} %copy-done.22, bf16[2,512,128]{2,1,0:T(8,128)(2,1)} %param.18), kind=kOutput, calls=%fused_computation.40 | convolution fusion | flops 3066036224 | bytes 8568832 | tf_op jit(solution)/shard_map/dot_general | solution.py:583
  439.6 9.1 %fusion.21.down_1 = f32[1376,128]{1,0:T(8,128)} fusion(bf16[2048,512]{1,0:T(8,128)(2,1)} %copy-done, bf16[2,512,128]{2,1,0:T(8,128)(2,1)} %param.19, bf16[2048,1376]{0,1:T(8,128)(2,1)} %copy-done.19), kind=kOutput, calls=%fused_computation.38 | convolution fusion | flops 3094216704 | bytes 8568832 | tf_op jit(solution)/shard_map/dot_general | solution.py:584
  448.7 1.7 collective-permute-start.11
  450.4 1.0 collective-permute-start.12
  451.4 6.4 %place.6.refs_4_ = bf16[512,32000]{1,0:T(8,128)(2,1)} custom-call(bf16[512,2048]{1,0:T(8,128)(2,1)} %collective-permute-done.7.refs_0_, bf16[512,2048]{1,0:T(8,128)(2,1)} %collective-permute-done.8.refs_1_, bf16[512,2048]{1,0:T(8,128)(2,1)} %collective-permute-done.9.refs_2_, ...), custom_call_target="tpu_custom_call", output_to_operand_aliasing={{}: (4, {})} | custom-call | flops 3000000000 | bytes 16777216 | tf_op jit(solution)/shard_map/place/pallas_call | solution.py:444
  457.9 0.0 copy-start.6
  457.9 0.0 copy-start.12
  457.9 66.3 %small_update.1 = (f32[4,172,128]{2,1,0:T(8,128)S(1)}, f32[4,172,128]{2,1,0:T(8,128)S(1)}, bf16[2,1376,128]{2,1,0:T(8,128)(2,1)S(1)}, bf16[2,1376,128]{2,1,0:T(8,128)(2,1)S(1)}) custom-call(f32[1376,128]{1,0:T(8,128)S(1)} %fusion.30.up_0, f32[1376,128]{1,0:T(8,128)S(1)} %copy-done.1, f32[1376,128]{1,0:T(8,128)S(1)} %copy-done.2, f32[1376,128]{1,0:T(8,128)S(1)} %copy-done.3, ...), custom_call_target="tpu_custom_call" | custom-call | flops 30000001024 | bytes 10000000 | tf_op jit(solution)/shard_map/small_update/pallas_call | solution.py:530
  524.2 0.0 copy-start.10
  524.2 0.0 copy-start.14
  524.2 0.0 collective-permute-done.11.refs_0_
  524.2 0.4 collective-permute-start.13
  524.6 0.1 collective-permute-start.14
  524.8 0.8 copy.31
  525.5 0.8 copy.29
  526.3 0.8 copy.32
  527.1 0.8 copy.30
  527.9 2.5 fusion.20
  530.3 2.5 subtract_convert_fusion
  532.8 0.0 collective-permute-done.13.refs_2_
  532.8 0.0 collective-permute-done.14.refs_3_
  532.8 4.0 place.7
  (51 shorter events, 0.2 us)
Async XLA Ops:
  1.7 9.2 %copy-start.7 = (bf16[2,1376,512]{2,1,0:T(8,128)(2,1)S(1)}, bf16[2,1376,512]{2,1,0:T(8,128)(2,1)}, u32[]{:S(2)}) copy-start(bf16[2,1376,512]{2,1,0:T(8,128)(2,1)} %param.16) | copy-start | bytes 8454148
  1.7 9.2 %copy-start.17 = (bf16[2048,512]{1,0:T(8,128)(2,1)S(1)}, bf16[2048,512]{1,0:T(8,128)(2,1)}, u32[]{:S(2)}) copy-start(bf16[2048,512]{1,0:T(8,128)(2,1)} %param.13) | copy-start | bytes 6291460
  1.8 24.6 %collective-permute-start = (f32[2,96,512]{2,1,0:T(8,128)S(1)}, f32[2,96,512]{2,1,0:T(8,128)S(1)}, u32[]{:S(2)}, u32[]{:S(2)}) collective-permute-start(f32[2,96,512]{2,1,0:T(8,128)S(1)} %pad_maximum_fusion), channel_id=1, source_target_pairs={{1,0},{2,1},{3,2},{4,3},{5,4},{6,5},{7,6}} | collective-permute-start | bytes 1179656 | tf_op jit(solution)/shard_map/ppermute | solution.py:557
  8.4 2.5 copy-start.20
  10.9 5.8 %copy-start.4 = (bf16[2,512,1376]{1,2,0:T(8,128)(2,1)S(1)}, bf16[2,512,1376]{1,2,0:T(8,128)(2,1)}, u32[]{:S(2)}) copy-start(bf16[2,512,1376]{1,2,0:T(8,128)(2,1)} %param.15) | copy-start | bytes 8454148
  16.7 3.4 copy-start.22
  20.1 6.3 %copy-start.19 = (bf16[2048,1376]{0,1:T(8,128)(2,1)}, bf16[2048,1376]{0,1:T(8,128)(2,1)S(1)}, u32[]{:S(2)}) copy-start(bf16[2048,1376]{0,1:T(8,128)(2,1)S(1)} %convolution_convert_fusion) | copy-start | bytes 16908292
  26.4 0.7 copy-start.18
  27.1 296.0 %copy-start.8 = (bf16[2,1376,512]{2,1,0:T(8,128)(2,1)S(1)}, bf16[2,1376,512]{2,1,0:T(8,128)(2,1)}, u32[]{:S(2)}) copy-start(bf16[2,1376,512]{2,1,0:T(8,128)(2,1)} %param.16) | copy-start | bytes 8454148
  323.1 13.0 %copy-start = (bf16[2048,512]{1,0:T(8,128)(2,1)}, bf16[2048,512]{1,0:T(8,128)(2,1)S(1)}, u32[]{:S(2)}) copy-start(bf16[2048,512]{1,0:T(8,128)(2,1)S(1)} %get-tuple-element.36) | copy-start | bytes 6291460
  323.1 13.0 %copy-start.5 = (bf16[2,512,1376]{1,2,0:T(8,128)(2,1)S(1)}, bf16[2,512,1376]{1,2,0:T(8,128)(2,1)}, u32[]{:S(2)}) copy-start(bf16[2,512,1376]{1,2,0:T(8,128)(2,1)} %param.15) | copy-start | bytes 8454148
  334.5 5.7 %copy-start.21 = (bf16[2048,1376]{0,1:T(8,128)(2,1)}, bf16[2048,1376]{0,1:T(8,128)(2,1)S(1)}, u32[]{:S(2)}) copy-start(bf16[2048,1376]{0,1:T(8,128)(2,1)S(1)} %fusion.4) | copy-start | bytes 16908292
  334.5 47.6 %collective-permute-start.1 = (bf16[512,2048]{1,0:T(8,128)(2,1)}, bf16[512,2048]{1,0:T(8,128)(2,1)S(1)}, u32[]{:S(2)}, u32[]{:S(2)}) collective-permute-start(bf16[512,2048]{1,0:T(8,128)(2,1)} %get-tuple-element.42.refs_0_), channel_id=1, source_target_pairs={{0,2},{1,3},{2,0},{3,1},{4,6},{5,7},{6,4},{7,5}} | collective-permute-start | bytes 6291464 | tf_op jit(solution)/shard_map/ppermute | solution.py:372
  335.6 4.6 slice-start
  335.6 4.6 copy-start.9
  335.6 4.7 slice-start.1
  335.6 47.4 %collective-permute-start.2 = (bf16[512,2048]{1,0:T(8,128)(2,1)}, bf16[512,2048]{1,0:T(8,128)(2,1)}, u32[]{:S(2)}, u32[]{:S(2)}) collective-permute-start(bf16[512,2048]{1,0:T(8,128)(2,1)} %get-tuple-element.43.refs_1_), channel_id=1, source_target_pairs={{0,4},{1,5},{2,6},{3,7},{4,0},{5,1},{6,2},{7,3}} | collective-permute-start | bytes 6291464 | tf_op jit(solution)/shard_map/ppermute | solution.py:372
  340.3 10.4 %copy-start.23 = (bf16[2048,512]{1,0:T(8,128)(2,1)}, bf16[2048,512]{1,0:T(8,128)(2,1)S(1)}, u32[]{:S(2)}) copy-start(bf16[2048,512]{1,0:T(8,128)(2,1)S(1)} %add_convert_fusion) | copy-start | bytes 6291460
  340.3 10.9 %copy-start.13 = (bf16[2,512,128]{2,1,0:T(8,128)(2,1)S(1)}, bf16[2,512,128]{2,1,0:T(8,128)(2,1)}, u32[]{:S(2)}) copy-start(bf16[2,512,128]{2,1,0:T(8,128)(2,1)} %param.19) | copy-start | bytes 786436
  350.6 9.6 %copy-start.11 = (bf16[2,512,128]{2,1,0:T(8,128)(2,1)S(1)}, bf16[2,512,128]{2,1,0:T(8,128)(2,1)}, u32[]{:S(2)}) copy-start(bf16[2,512,128]{2,1,0:T(8,128)(2,1)} %param.18) | copy-start | bytes 786436
  350.6 33.2 %collective-permute-start.5 = (bf16[512,2048]{1,0:T(8,128)(2,1)}, bf16[512,2048]{1,0:T(8,128)(2,1)}, u32[]{:S(2)}, u32[]{:S(2)}) collective-permute-start(bf16[512,2048]{1,0:T(8,128)(2,1)} %get-tuple-element.42.refs_0_), channel_id=1, source_target_pairs={{0,1},{1,0},{2,3},{3,2},{4,5},{5,4},{6,7},{7,6}} | collective-permute-start | bytes 6291464 | tf_op jit(solution)/shard_map/ppermute | solution.py:372
  350.6 36.2 %collective-permute-start.6 = (bf16[512,2048]{1,0:T(8,128)(2,1)}, bf16[512,2048]{1,0:T(8,128)(2,1)}, u32[]{:S(2)}, u32[]{:S(2)}) collective-permute-start(bf16[512,2048]{1,0:T(8,128)(2,1)} %get-tuple-element.43.refs_1_), channel_id=1, source_target_pairs={{0,1},{1,0},{2,3},{3,2},{4,5},{5,4},{6,7},{7,6}} | collective-permute-start | bytes 6291464 | tf_op jit(solution)/shard_map/ppermute | solution.py:372
  360.2 24.6 %copy-start.15 = (f32[2,128,172]{1,0,2:T(2,128)S(1)}, f32[2,128,172]{1,0,2:T(2,128)}, u32[]{:S(2)}) copy-start(f32[2,128,172]{1,0,2:T(2,128)} %param.20) | copy-start | bytes 528388
  360.2 24.6 %copy-start.16 = (f32[2,128,172]{1,0,2:T(2,128)S(1)}, f32[2,128,172]{1,0,2:T(2,128)}, u32[]{:S(2)}) copy-start(f32[2,128,172]{1,0,2:T(2,128)} %param.21) | copy-start | bytes 528388
  383.0 26.1 %collective-permute-start.3 = (bf16[512,2048]{1,0:T(8,128)(2,1)S(1)}, bf16[512,2048]{1,0:T(8,128)(2,1)S(1)}, u32[]{:S(2)}, u32[]{:S(2)}) collective-permute-start(bf16[512,2048]{1,0:T(8,128)(2,1)S(1)} %collective-permute-done.1.refs_0_), channel_id=1, source_target_pairs={{0,1},{1,0},{2,3},{3,2},{4,5},{5,4},{6,7},{7,6}} | collective-permute-start | bytes 6291464 | tf_op jit(solution)/shard_map/ppermute | solution.py:372
  383.0 26.1 %collective-permute-start.4 = (bf16[512,2048]{1,0:T(8,128)(2,1)}, bf16[512,2048]{1,0:T(8,128)(2,1)S(1)}, u32[]{:S(2)}, u32[]{:S(2)}) collective-permute-start(bf16[512,2048]{1,0:T(8,128)(2,1)} %collective-permute-done.2.refs_1_), channel_id=1, source_target_pairs={{0,1},{1,0},{2,3},{3,2},{4,5},{5,4},{6,7},{7,6}} | collective-permute-start | bytes 6291464 | tf_op jit(solution)/shard_map/ppermute | solution.py:372
  383.5 47.9 %collective-permute-start.7 = (bf16[512,2048]{1,0:T(8,128)(2,1)}, bf16[512,2048]{1,0:T(8,128)(2,1)}, u32[]{:S(2)}, u32[]{:S(2)}) collective-permute-start(bf16[512,2048]{1,0:T(8,128)(2,1)} %get-tuple-element.42.refs_0_), channel_id=1, source_target_pairs={{0,4},{1,5},{2,6},{3,7},{4,0},{5,1},{6,2},{7,3}} | collective-permute-start | bytes 6291464 | tf_op jit(solution)/shard_map/ppermute | solution.py:372
  383.8 47.6 %collective-permute-start.8 = (bf16[512,2048]{1,0:T(8,128)(2,1)}, bf16[512,2048]{1,0:T(8,128)(2,1)}, u32[]{:S(2)}, u32[]{:S(2)}) collective-permute-start(bf16[512,2048]{1,0:T(8,128)(2,1)} %get-tuple-element.43.refs_1_), channel_id=1, source_target_pairs={{0,2},{1,3},{2,0},{3,1},{4,6},{5,7},{6,4},{7,5}} | collective-permute-start | bytes 6291464 | tf_op jit(solution)/shard_map/ppermute | solution.py:372
  431.4 20.0 %collective-permute-start.9 = (bf16[512,2048]{1,0:T(8,128)(2,1)}, bf16[512,2048]{1,0:T(8,128)(2,1)}, u32[]{:S(2)}, u32[]{:S(2)}) collective-permute-start(bf16[512,2048]{1,0:T(8,128)(2,1)} %collective-permute-done.7.refs_0_), channel_id=1, source_target_pairs={{0,1},{1,0},{2,3},{3,2},{4,5},{5,4},{6,7},{7,6}} | collective-permute-start | bytes 6291464 | tf_op jit(solution)/shard_map/ppermute | solution.py:372
  431.4 20.0 %collective-permute-start.10 = (bf16[512,2048]{1,0:T(8,128)(2,1)}, bf16[512,2048]{1,0:T(8,128)(2,1)}, u32[]{:S(2)}, u32[]{:S(2)}) collective-permute-start(bf16[512,2048]{1,0:T(8,128)(2,1)} %collective-permute-done.8.refs_1_), channel_id=1, source_target_pairs={{0,1},{1,0},{2,3},{3,2},{4,5},{5,4},{6,7},{7,6}} | collective-permute-start | bytes 6291464 | tf_op jit(solution)/shard_map/ppermute | solution.py:372
  448.7 9.2 %copy-start.1 = (f32[1376,128]{1,0:T(8,128)S(1)}, f32[1376,128]{1,0:T(8,128)}, u32[]{:S(2)}) copy-start(f32[1376,128]{1,0:T(8,128)} %fusion.24.up_1) | copy-start | bytes 2113540
  448.7 9.2 %copy-start.2 = (f32[1376,128]{1,0:T(8,128)S(1)}, f32[1376,128]{1,0:T(8,128)}, u32[]{:S(2)}) copy-start(f32[1376,128]{1,0:T(8,128)} %fusion.27.down_0) | copy-start | bytes 2113540
  448.7 9.2 %copy-start.3 = (f32[1376,128]{1,0:T(8,128)S(1)}, f32[1376,128]{1,0:T(8,128)}, u32[]{:S(2)}) copy-start(f32[1376,128]{1,0:T(8,128)} %fusion.21.down_1) | copy-start | bytes 2113540
  448.7 75.5 %collective-permute-start.11 = (bf16[512,2048]{1,0:T(8,128)(2,1)S(1)}, bf16[512,2048]{1,0:T(8,128)(2,1)S(1)}, u32[]{:S(2)}, u32[]{:S(2)}) collective-permute-start(bf16[512,2048]{1,0:T(8,128)(2,1)S(1)} %collective-permute-done.1.refs_0_), channel_id=1, source_target_pairs={{0,4},{1,5},{2,6},{3,7},{4,0},{5,1},{6,2},{7,3}} | collective-permute-start | bytes 6291464 | tf_op jit(solution)/shard_map/ppermute | solution.py:372
  450.4 73.8 %collective-permute-start.12 = (bf16[512,2048]{1,0:T(8,128)(2,1)}, bf16[512,2048]{1,0:T(8,128)(2,1)S(1)}, u32[]{:S(2)}, u32[]{:S(2)}) collective-permute-start(bf16[512,2048]{1,0:T(8,128)(2,1)} %collective-permute-done.2.refs_1_), channel_id=1, source_target_pairs={{0,2},{1,3},{2,0},{3,1},{4,6},{5,7},{6,4},{7,5}} | collective-permute-start | bytes 6291464 | tf_op jit(solution)/shard_map/ppermute | solution.py:372
  457.9 70.0 %copy-start.6 = (bf16[2,512,1376]{1,2,0:T(8,128)(2,1)S(1)}, bf16[2,512,1376]{1,2,0:T(8,128)(2,1)}, u32[]{:S(2)}) copy-start(bf16[2,512,1376]{1,2,0:T(8,128)(2,1)} %param.15) | copy-start | bytes 8454148
  457.9 70.0 %copy-start.12 = (bf16[2,512,128]{2,1,0:T(8,128)(2,1)S(1)}, bf16[2,512,128]{2,1,0:T(8,128)(2,1)}, u32[]{:S(2)}) copy-start(bf16[2,512,128]{2,1,0:T(8,128)(2,1)} %param.18) | copy-start | bytes 786436
  524.2 6.1 %copy-start.10 = (bf16[2,1376,512]{2,1,0:T(8,128)(2,1)S(1)}, bf16[2,1376,512]{2,1,0:T(8,128)(2,1)}, u32[]{:S(2)}) copy-start(bf16[2,1376,512]{2,1,0:T(8,128)(2,1)} %param.16) | copy-start | bytes 8454148
  524.2 6.1 %copy-start.14 = (bf16[2,512,128]{2,1,0:T(8,128)(2,1)S(1)}, bf16[2,512,128]{2,1,0:T(8,128)(2,1)}, u32[]{:S(2)}) copy-start(bf16[2,512,128]{2,1,0:T(8,128)(2,1)} %param.19) | copy-start | bytes 786436
  524.2 8.6 %collective-permute-start.13 = (bf16[512,2048]{1,0:T(8,128)(2,1)S(1)}, bf16[512,2048]{1,0:T(8,128)(2,1)S(1)}, u32[]{:S(2)}, u32[]{:S(2)}) collective-permute-start(bf16[512,2048]{1,0:T(8,128)(2,1)S(1)} %collective-permute-done.11.refs_0_), channel_id=1, source_target_pairs={{0,1},{1,0},{2,3},{3,2},{4,5},{5,4},{6,7},{7,6}} | collective-permute-start | bytes 6291464 | tf_op jit(solution)/shard_map/ppermute | solution.py:372
  524.6 8.2 %collective-permute-start.14 = (bf16[512,2048]{1,0:T(8,128)(2,1)S(1)}, bf16[512,2048]{1,0:T(8,128)(2,1)S(1)}, u32[]{:S(2)}, u32[]{:S(2)}) collective-permute-start(bf16[512,2048]{1,0:T(8,128)(2,1)S(1)} %collective-permute-done.12.refs_1_), channel_id=1, source_target_pairs={{0,1},{1,0},{2,3},{3,2},{4,5},{5,4},{6,7},{7,6}} | collective-permute-start | bytes 6291464 | tf_op jit(solution)/shard_map/ppermute | solution.py:372
